TPU v7x, 256 devices: a whole 4x4x8 slice. The times are simulated.
256 devices in a mesh: src: 8 (over z), tgt: 32 (over x, y, core).
Axes of the slice: x: 4, y: 4, z: 8, core: 2. Of those that a mesh axis runs over, the one named last changes fastest.
Arguments:
- generator: int32 [64], replicated, may hold values from 1 to 16383, as said below
- shift: float32 [64], replicated, may hold values from 0 to 1
- targets: float32 [64, 32768], P(None, 'tgt'), may hold values from -8 to 8
- log_weights: float32 [32768], P('tgt'), may hold values from -20 to 150
Outputs:
- potential_f: float32 [16384], P('src')
- potential_g: float32 [32768], P('tgt')
Inputs may be any that keep to these rules, and one draw needn't show every extreme that they name: `generator`: odd integers.
All inputs are finite; a program needn't handle non-finite values.
Results may differ from a plain program's by a relative error of at most 0.0003.
Values sent between devices are 32-bit elements; how exact they have to be, the bound alone decides.
No kernel may reach another device: no remote copies, remote signals or barrier semaphores. Data moves between devices by JAX's collectives and lax.ppermute only.
A program may use at most 64 MiB of HBM per device.

v0:
```python
import jax
import jax.numpy as jnp
from jax import lax
from jax.sharding import PartitionSpec as P

SRC_DEV = 2048
ITERS = 2


blur_level = 0.1
highest = lax.Precision.HIGHEST


def from_everyone(x, axis):
    copies = jnp.broadcast_to(x, (lax.axis_size(axis), *x.shape))
    return lax.all_to_all(copies, axis, split_axis=0, concat_axis=0, tiled=True)


def gathered_once(x, axis):
    leaves = jax.tree.leaves(x)
    order = sorted(range(len(leaves)), key=lambda k: -leaves[k].size)
    width = (1, *leaves[order[0]].shape)[-1]
    lines = [
        jnp.pad(leaves[k].reshape(-1), (0, -leaves[k].size % width)).reshape(-1, width)
        for k in order
    ]
    both, at, found = (from_everyone(jnp.concatenate(lines), axis), 0, {})
    for k, line in zip(order, lines):
        slab = both[:, at : at + len(line)].reshape(len(both), -1)
        found[k] = slab[:, : leaves[k].size].reshape(-1, *leaves[k].shape)
        at += len(line)
    numbers = iter(range(len(leaves)))
    return jax.tree.map(lambda _: found[next(numbers)], x)


def combined_pairwise(pieces, combine):
    while len(jax.tree.leaves(pieces)[0]) > 1:
        pieces = jax.vmap(combine)(
            *(jax.tree.map(lambda part: part[side::2], pieces) for side in (0, 1))
        )
    return jax.tree.map(lambda part: part[0], pieces)


def combined_all(x, axis, combine):
    pieces = gathered_once(x, axis)
    return combined_pairwise(pieces, combine)


def once_a_type(x, axis):
    leaves, found = (jax.tree.leaves(x), {})
    for leading, a in enumerate(leaves):
        if leading not in found:
            alike = [k for k, b in enumerate(leaves) if b.dtype == a.dtype]
            got = (
                gathered_once([leaves[k] for k in alike], axis)
                if len(alike) > 1
                else [from_everyone(a, axis)]
            )
            for k, b in zip(alike, got):
                found[k] = b
    numbers = iter(range(len(leaves)))
    return jax.tree.map(lambda _: found[next(numbers)], x)


def merged(x, axis, combine):
    pieces = once_a_type(x, axis)
    return combined_pairwise(pieces, combine)


def pair_combine(first, second):
    top = jnp.maximum(first[0], second[0])
    return (top, first[1] * jnp.exp(first[0] - top) + second[1] * jnp.exp(second[0] - top))


def lattice_block(generator, shift, start, count, modulus):
    index = start + jnp.arange(count, dtype=jnp.int32)
    folded = index[None, :] * generator[:, None] % modulus
    phase = folded.astype(jnp.float32) / modulus + shift[:, None]
    return jnp.sin(2.0 * jnp.pi * phase)


def cost_block(points, targets, far):
    cross = lax.dot_general(
        points,
        targets,
        (((0,), (0,)), ((), ())),
        precision=highest,
        preferred_element_type=jnp.float32,
    )
    near = 0.5 * jnp.sum(points * points, 0)
    return near[:, None] + far[None, :] - cross


def weight_reduce(peak, total):
    return combined_all((peak, total), "tgt", pair_combine)


def row_reduce(peak, total):
    top, summed = merged((peak, total), "tgt", pair_combine)
    return -blur_level * (top + jnp.log(summed))


def column_reduce(peak, total):
    top, summed = combined_all((peak, total), "src", pair_combine)
    return -blur_level * (top + jnp.log(summed))


def local(generator, shift, targets, log_weights):
    modulus = SRC_DEV * lax.axis_size("src")
    offset = lax.axis_index("src") * SRC_DEV
    block = min(512, SRC_DEV)
    count = SRC_DEV // block
    local_peak = jnp.max(log_weights)
    local_total = jnp.sum(jnp.exp(log_weights - local_peak))
    weight_top, weight_sum = weight_reduce(local_peak, local_total)
    log_b = log_weights - (weight_top + jnp.log(weight_sum))
    log_a = -jnp.log(jnp.float32(modulus))
    far = 0.5 * jnp.sum(targets * targets, 0)
    columns = targets.shape[1]
    potential_g = jnp.zeros((columns,), jnp.float32)
    potential_f = jnp.zeros((SRC_DEV,), jnp.float32)
    for step in range(ITERS):

        def row_pass(index, current_g=potential_g):
            points = lattice_block(generator, shift, offset + index * block, block, modulus)
            scores = (
                log_b[None, :]
                + (current_g[None, :] - cost_block(points, targets, far)) / blur_level
            )
            top = jnp.max(scores, 1)
            return (top, jnp.sum(jnp.exp(scores - top[:, None]), 1))

        peaks, totals = lax.map(row_pass, jnp.arange(count, dtype=jnp.int32))
        potential_f = row_reduce(peaks.reshape(SRC_DEV), totals.reshape(SRC_DEV))

        def column_pass(carry, index, current_f=potential_f):
            peak_c, total_c = carry
            start = index * block
            points = lattice_block(generator, shift, offset + start, block, modulus)
            part = lax.dynamic_slice_in_dim(current_f, start, block)
            scores = log_a + (part[:, None] - cost_block(points, targets, far)) / blur_level
            top = jnp.maximum(peak_c, jnp.max(scores, 0))
            total = total_c * jnp.exp(peak_c - top) + jnp.sum(jnp.exp(scores - top[None, :]), 0)
            return ((top, total), None)

        start_carry = (jnp.full((columns,), -1e30, jnp.float32), jnp.zeros((columns,), jnp.float32))
        (top, total), unused = lax.scan(
            column_pass, start_carry, jnp.arange(count, dtype=jnp.int32)
        )
        potential_g = column_reduce(top, total)
    return (potential_f, potential_g)


def solution(mesh):
    in_specs = (P(), P(), P(None, "tgt"), P("tgt"))
    out_specs = (P("src"), P("tgt"))
    return jax.shard_map(local, mesh=mesh, in_specs=in_specs, out_specs=out_specs, check_vma=False)
```

profile of v0, /device:TPU:1, one launch (start us, length us, event | category | flops | bytes accessed | tf_op | source)
XLA Modules:
  0.0 183.4 jit_solution(470360761426393353)
XLA Ops:
  5.8 8.6 %all-to-all-start = ((f32[32,2,1]{1,2,0:T(1,128)}), f32[32,2,1]{1,2,0:T(1,128)S(1)}, u32[]{:S(2)}, u32[]{:S(2)}) async-start(f32[32,2,1]{1,2,0:T(1,128)} %broadcast_in_dim.64), calls=%async_computation | async-start | bytes 32768 | tf_op jit(solution)/shard_map/all_to_all | solution.py:16
  15.4 6.0 %all-to-all-done = f32[32,2,1]{1,2,0:T(1,128)S(1)} async-done(((f32[32,2,1]{1,2,0:T(1,128)}), f32[32,2,1]{1,2,0:T(1,128)S(1)}, u32[]{:S(2)}, u32[]{:S(2)}) %all-to-all-start) | async-done | bytes 288 | tf_op jit(solution)/shard_map/all_to_all | solution.py:16
  28.8 27.8 %while.58 = (s32[]{:T(128)}, f32[4,512]{1,0:T(4,128)S(1)}, f32[4,512]{1,0:T(4,128)S(1)}, f32[1024]{0:T(1024)S(1)}, s32[4]{0:T(128)S(1)}, /*index=5*/s32[]{:T(128...) while((s32[]{:T(128)}, f32[4,512]{1,0:T(4,128)S(1)}, ...), condition=%wide.region_7.8_spmd, body=%wide.region_3.7_spmd.sunk | while | flops 407961088 | bytes 4494509 | solution.py:133
  31.4 3.8 %fusion.83 = (f32[512]{0:T(512)S(1)}, f32[512,1024]{1,0:T(8,128)S(1)}) fusion(f32[64,1024]{1,0:T(8,128)} %get-tuple-element.1035, f32[64]{0:T(128)} %get-tuple-element.1033, s32[64]{0:T(128)} %get-tuple-element.1032, s32[512]{0:T(512)S(1)} %iota_add_fusion.8, f32[1024]{0:T(1024)S(1)} %get-tuple-element.1034, f32[512]{0:T(512)S(1)} %broadcast_multiply_fusion.9, ...), kind=kOutput, calls=%fused_computation.149.clone.1 | convolution fusion | flops 406322688 | bytes 2374144 | tf_op jit(solution)/shard_map/while/body/eval_jaxpr/dot_general | solution.py:83
  38.3 3.8 %fusion.83 = (f32[512]{0:T(512)S(1)}, f32[512,1024]{1,0:T(8,128)S(1)}) fusion(f32[64,1024]{1,0:T(8,128)} %get-tuple-element.1035, f32[64]{0:T(128)} %get-tuple-element.1033, s32[64]{0:T(128)} %get-tuple-element.1032, s32[512]{0:T(512)S(1)} %iota_add_fusion.8, f32[1024]{0:T(1024)S(1)} %get-tuple-element.1034, f32[512]{0:T(512)S(1)} %broadcast_multiply_fusion.9, ...), kind=kOutput, calls=%fused_computation.149.clone.1 | convolution fusion | flops 406322688 | bytes 2374144 | tf_op jit(solution)/shard_map/while/body/eval_jaxpr/dot_general | solution.py:83
  45.2 3.8 %fusion.83 = (f32[512]{0:T(512)S(1)}, f32[512,1024]{1,0:T(8,128)S(1)}) fusion(f32[64,1024]{1,0:T(8,128)} %get-tuple-element.1035, f32[64]{0:T(128)} %get-tuple-element.1033, s32[64]{0:T(128)} %get-tuple-element.1032, s32[512]{0:T(512)S(1)} %iota_add_fusion.8, f32[1024]{0:T(1024)S(1)} %get-tuple-element.1034, f32[512]{0:T(512)S(1)} %broadcast_multiply_fusion.9, ...), kind=kOutput, calls=%fused_computation.149.clone.1 | convolution fusion | flops 406322688 | bytes 2374144 | tf_op jit(solution)/shard_map/while/body/eval_jaxpr/dot_general | solution.py:83
  52.2 3.8 %fusion.83 = (f32[512]{0:T(512)S(1)}, f32[512,1024]{1,0:T(8,128)S(1)}) fusion(f32[64,1024]{1,0:T(8,128)} %get-tuple-element.1035, f32[64]{0:T(128)} %get-tuple-element.1033, s32[64]{0:T(128)} %get-tuple-element.1032, s32[512]{0:T(512)S(1)} %iota_add_fusion.8, f32[1024]{0:T(1024)S(1)} %get-tuple-element.1034, f32[512]{0:T(512)S(1)} %broadcast_multiply_fusion.9, ...), kind=kOutput, calls=%fused_computation.149.clone.1 | convolution fusion | flops 406322688 | bytes 2374144 | tf_op jit(solution)/shard_map/while/body/eval_jaxpr/dot_general | solution.py:83
  57.6 4.2 %all-to-all-start.1 = ((f32[32,2,2048]{2,1,0:T(2,128)}), f32[32,2,2048]{2,1,0:T(2,128)S(1)}, u32[]{:S(2)}, u32[]{:S(2)}) async-start(f32[32,2,2048]{2,1,0:T(2,128)} %broadcast_in_dim.70), calls=%async_computation.1 | async-start | bytes 1048576 | tf_op jit(solution)/shard_map/all_to_all | solution.py:16
  61.9 11.7 %all-to-all-done.1 = f32[32,2,2048]{2,1,0:T(2,128)S(1)} async-done(((f32[32,2,2048]{2,1,0:T(2,128)}), f32[32,2,2048]{2,1,0:T(2,128)S(1)}, u32[]{:S(2)}, u32[]{:S(2)}) %all-to-all-start.1) | async-done | bytes 524320 | tf_op jit(solution)/shard_map/all_to_all | solution.py:16
  75.0 20.1 %while.60 = (s32[]{:T(128)}, f32[1024]{0:T(1024)S(1)}, f32[1024]{0:T(1024)S(1)}, s32[4]{0:T(128)S(1)}, f32[2048]{0:T(1024)S(1)}, /*index=5*/s32[]{:T(128)}, s32[...) while((s32[]{:T(128)}, f32[1024]{0:T(1024)S(1)}, ...), condition=%wide.region_12.13_spmd.clone, body=%wide.region_8.12_spmd.clone.sunk | while | flops 407967232 | bytes 4535518 | solution.py:147
  77.0 2.7 %fusion.87 = (f32[1024]{0:T(1024)S(1)}, f32[512,1024]{1,0:T(8,128)S(1)}) fusion(f32[64,1024]{1,0:T(8,128)S(1)} %get-tuple-element.1076, f32[64]{0:T(128)S(1)} %get-tuple-element.1074, s32[64]{0:T(128)S(1)} %get-tuple-element.1073, s32[512]{0:T(512)S(1)} %iota_add_fusion.10, f32[1024]{0:T(1024)S(1)} %get-tuple-element.1075, ...), kind=kOutput, calls=%fused_computation.151.clone.1 | convolution fusion | flops 406322176 | bytes 2374144 | tf_op jit(solution)/shard_map/while/body/eval_jaxpr/dot_general | solution.py:83
  87.1 2.7 %fusion.87 = (f32[1024]{0:T(1024)S(1)}, f32[512,1024]{1,0:T(8,128)S(1)}) fusion(f32[64,1024]{1,0:T(8,128)S(1)} %get-tuple-element.1076, f32[64]{0:T(128)S(1)} %get-tuple-element.1074, s32[64]{0:T(128)S(1)} %get-tuple-element.1073, s32[512]{0:T(512)S(1)} %iota_add_fusion.10, f32[1024]{0:T(1024)S(1)} %get-tuple-element.1075, ...), kind=kOutput, calls=%fused_computation.151.clone.1 | convolution fusion | flops 406322176 | bytes 2374144 | tf_op jit(solution)/shard_map/while/body/eval_jaxpr/dot_general | solution.py:83
  95.9 8.2 %all-to-all-start.2 = ((f32[8,2,1024]{2,1,0:T(2,128)}), f32[8,2,1024]{2,1,0:T(2,128)S(1)}, u32[]{:S(2)}, u32[]{:S(2)}) async-start(f32[8,2,1024]{2,1,0:T(2,128)} %broadcast_in_dim.71), calls=%async_computation.2 | async-start | bytes 131072 | tf_op jit(solution)/shard_map/all_to_all | solution.py:16
  104.0 7.4 %all-to-all-done.2 = f32[8,2,1024]{2,1,0:T(2,128)S(1)} async-done(((f32[8,2,1024]{2,1,0:T(2,128)}), f32[8,2,1024]{2,1,0:T(2,128)S(1)}, u32[]{:S(2)}, u32[]{:S(2)}) %all-to-all-start.2) | async-done | bytes 65568 | tf_op jit(solution)/shard_map/all_to_all | solution.py:16
  111.9 21.2 %while.59 = (s32[]{:T(128)}, f32[4,512]{1,0:T(4,128)S(1)}, f32[4,512]{1,0:T(4,128)S(1)}, f32[1024]{0:T(1024)S(1)}, f32[1024]{0:T(1024)S(1)}, /*index=5*/s32[4]{0...) while((s32[]{:T(128)}, f32[4,512]{1,0:T(4,128)S(1)}, ...), condition=%wide.region_17.18_spmd, body=%wide.region_13.17_spmd.sunk | while | flops 407961088 | bytes 4498613 | solution.py:133
  113.7 2.8 %fusion.85 = (f32[512]{0:T(512)S(1)}, f32[512,1024]{1,0:T(8,128)S(1)}) fusion(f32[64,1024]{1,0:T(8,128)S(1)} %get-tuple-element.1119, f32[64]{0:T(128)S(1)} %get-tuple-element.1117, s32[64]{0:T(128)S(1)} %get-tuple-element.1116, s32[512]{0:T(512)S(1)} %iota_add_fusion.9, f32[1024]{0:T(1024)S(1)} %get-tuple-element.1118, ...), kind=kOutput, calls=%fused_computation.150.clone.1 | convolution fusion | flops 406322688 | bytes 2378240 | tf_op jit(solution)/shard_map/while/body/eval_jaxpr/dot_general | solution.py:83
  119.0 2.8 %fusion.85 = (f32[512]{0:T(512)S(1)}, f32[512,1024]{1,0:T(8,128)S(1)}) fusion(f32[64,1024]{1,0:T(8,128)S(1)} %get-tuple-element.1119, f32[64]{0:T(128)S(1)} %get-tuple-element.1117, s32[64]{0:T(128)S(1)} %get-tuple-element.1116, s32[512]{0:T(512)S(1)} %iota_add_fusion.9, f32[1024]{0:T(1024)S(1)} %get-tuple-element.1118, ...), kind=kOutput, calls=%fused_computation.150.clone.1 | convolution fusion | flops 406322688 | bytes 2378240 | tf_op jit(solution)/shard_map/while/body/eval_jaxpr/dot_general | solution.py:83
  124.3 2.8 %fusion.85 = (f32[512]{0:T(512)S(1)}, f32[512,1024]{1,0:T(8,128)S(1)}) fusion(f32[64,1024]{1,0:T(8,128)S(1)} %get-tuple-element.1119, f32[64]{0:T(128)S(1)} %get-tuple-element.1117, s32[64]{0:T(128)S(1)} %get-tuple-element.1116, s32[512]{0:T(512)S(1)} %iota_add_fusion.9, f32[1024]{0:T(1024)S(1)} %get-tuple-element.1118, ...), kind=kOutput, calls=%fused_computation.150.clone.1 | convolution fusion | flops 406322688 | bytes 2378240 | tf_op jit(solution)/shard_map/while/body/eval_jaxpr/dot_general | solution.py:83
  129.6 2.8 %fusion.85 = (f32[512]{0:T(512)S(1)}, f32[512,1024]{1,0:T(8,128)S(1)}) fusion(f32[64,1024]{1,0:T(8,128)S(1)} %get-tuple-element.1119, f32[64]{0:T(128)S(1)} %get-tuple-element.1117, s32[64]{0:T(128)S(1)} %get-tuple-element.1116, s32[512]{0:T(512)S(1)} %iota_add_fusion.9, f32[1024]{0:T(1024)S(1)} %get-tuple-element.1118, ...), kind=kOutput, calls=%fused_computation.150.clone.1 | convolution fusion | flops 406322688 | bytes 2378240 | tf_op jit(solution)/shard_map/while/body/eval_jaxpr/dot_general | solution.py:83
  134.1 4.8 %all-to-all-start.3 = ((f32[32,2,2048]{2,1,0:T(2,128)}), f32[32,2,2048]{2,1,0:T(2,128)S(1)}, u32[]{:S(2)}, u32[]{:S(2)}) async-start(f32[32,2,2048]{2,1,0:T(2,128)} %broadcast_in_dim.72), calls=%async_computation.3 | async-start | bytes 1048576 | tf_op jit(solution)/shard_map/all_to_all | solution.py:16
  139.0 11.6 %all-to-all-done.3 = f32[32,2,2048]{2,1,0:T(2,128)S(1)} async-done(((f32[32,2,2048]{2,1,0:T(2,128)}), f32[32,2,2048]{2,1,0:T(2,128)S(1)}, u32[]{:S(2)}, u32[]{:S(2)}) %all-to-all-start.3) | async-done | bytes 524320 | tf_op jit(solution)/shard_map/all_to_all | solution.py:16
  152.0 20.1 %while.61 = (s32[]{:T(128)}, f32[1024]{0:T(1024)S(1)}, f32[1024]{0:T(1024)S(1)}, s32[4]{0:T(128)S(1)}, f32[2048]{0:T(1024)S(1)}, /*index=5*/s32[]{:T(128)}, s32[...) while((s32[]{:T(128)}, f32[1024]{0:T(1024)S(1)}, ...), condition=%wide.region_22.23_spmd.clone, body=%wide.region_18.22_spmd.clone.sunk | while | flops 407967232 | bytes 4535518 | solution.py:147
  159.0 2.7 %fusion.90 = (f32[1024]{0:T(1024)S(1)}, f32[512,1024]{1,0:T(8,128)S(1)}) fusion(f32[64,1024]{1,0:T(8,128)S(1)} %get-tuple-element.1160, f32[64]{0:T(128)S(1)} %get-tuple-element.1158, s32[64]{0:T(128)S(1)} %get-tuple-element.1157, s32[512]{0:T(512)S(1)} %iota_add_fusion.11, f32[1024]{0:T(1024)S(1)} %get-tuple-element.1159, ...), kind=kOutput, calls=%fused_computation.152.clone.1 | convolution fusion | flops 406322176 | bytes 2374144 | tf_op jit(solution)/shard_map/while/body/eval_jaxpr/dot_general | solution.py:83
  172.2 10.2 %all_to_all.25 = f32[8,2,1024]{2,1,0:T(2,128)S(1)} all-to-all(f32[8,2,1024]{2,1,0:T(2,128)S(1)} %broadcast_in_dim.73), channel_id=1, replica_groups=mesh['src'=8,'tgt'=32] {'src'}, dimensions={0} | all-to-all | bytes 131072 | tf_op jit(solution)/shard_map/all_to_all | solution.py:16
  (270 shorter events, 60.2 us)
Async XLA Ops:
  5.8 15.6 %all-to-all-start = ((f32[32,2,1]{1,2,0:T(1,128)}), f32[32,2,1]{1,2,0:T(1,128)S(1)}, u32[]{:S(2)}, u32[]{:S(2)}) async-start(f32[32,2,1]{1,2,0:T(1,128)} %broadcast_in_dim.64), calls=%async_computation | async-start | bytes 32768 | tf_op jit(solution)/shard_map/all_to_all | solution.py:16
  57.6 15.9 %all-to-all-start.1 = ((f32[32,2,2048]{2,1,0:T(2,128)}), f32[32,2,2048]{2,1,0:T(2,128)S(1)}, u32[]{:S(2)}, u32[]{:S(2)}) async-start(f32[32,2,2048]{2,1,0:T(2,128)} %broadcast_in_dim.70), calls=%async_computation.1 | async-start | bytes 1048576 | tf_op jit(solution)/shard_map/all_to_all | solution.py:16
  74.1 1.0 copy-start
  74.1 1.0 copy-start.2
  74.1 1.0 copy-start.3
  95.9 15.6 %all-to-all-start.2 = ((f32[8,2,1024]{2,1,0:T(2,128)}), f32[8,2,1024]{2,1,0:T(2,128)S(1)}, u32[]{:S(2)}, u32[]{:S(2)}) async-start(f32[8,2,1024]{2,1,0:T(2,128)} %broadcast_in_dim.71), calls=%async_computation.2 | async-start | bytes 131072 | tf_op jit(solution)/shard_map/all_to_all | solution.py:16
  134.1 16.5 %all-to-all-start.3 = ((f32[32,2,2048]{2,1,0:T(2,128)}), f32[32,2,2048]{2,1,0:T(2,128)S(1)}, u32[]{:S(2)}, u32[]{:S(2)}) async-start(f32[32,2,2048]{2,1,0:T(2,128)} %broadcast_in_dim.72), calls=%async_computation.3 | async-start | bytes 1048576 | tf_op jit(solution)/shard_map/all_to_all | solution.py:16
  172.2 11.2 %copy-start.1 = (f32[2048]{0:T(1024)}, f32[2048]{0:T(1024)S(1)}, u32[]{:S(2)}) copy-start(f32[2048]{0:T(1024)S(1)} %get-tuple-element.1172) | copy-start | bytes 24580
where the time goes:
time: 184 us; the launch traced here: 183 us
  matrix products  47.9 us (26%)
  waiting for transfers between devices  36.7 us (20%)
  other arithmetic  27 us (15%)
  starting transfers between devices  25.8 us (14%)
  local copies, waits for them, and re-layouts  19.7 us (11%)
  loops' own time  11.1 us (6%)
  blocking collectives  10.2 us (6%)
  between operations  5.09 us (3%)
    dot_general x16, matrix products, cost_block(): lax.dot_general(points, targets, (((0,), (0,)), ((), ())), precision=high...  47.9 us
    all_to_all x4, waiting for transfers between devices, from_everyone(): return lax.all_to_all(copies, axis, split_axis=0, concat_axis=0, tiled=True)  36.7 us
    all_to_all x4, starting transfers between devices, from_everyone(): return lax.all_to_all(copies, axis, split_axis=0, concat_axis=0, tiled=True)  25.8 us
    reduce_sum x16, other arithmetic, cost_block(): near = 0.5 * jnp.sum(points * points, 0)  12.4 us
    all_to_all x1, blocking collectives, from_everyone(): return lax.all_to_all(copies, axis, split_axis=0, concat_axis=0, tiled=True)  10.2 us
    dynamic_slice x16, local copies, waits for them, and re-layouts, local(): peaks, totals = lax.map(row_pass, jnp.arange(count, dtype=jnp.int32))  9.38 us
    another operation x2, loops' own time, local(): lax.scan(column_pass, start_carry, jnp.arange(count, dtype=jnp.int32))  5.63 us
    another operation x2, loops' own time, local(): peaks, totals = lax.map(row_pass, jnp.arange(count, dtype=jnp.int32))  5.51 us
  transfers between devices with their start and end apart: 4, of which 4 were waited for; matrix products, arithmetic and copies ran while one was open for 1% of the time, Pallas kernels for 0%

commit v1 on v0

v1 whole, which is shorter than its diff:
```python
import math
import jax
import jax.numpy as jnp
from jax import lax
from jax.experimental import pallas as pl
from jax.experimental.pallas import tpu as pltpu
from jax.sharding import PartitionSpec as P

DIM = 64
NSRC = 2048
NTGT = 1024
LANES = 128
SRC_TILES = NSRC // LANES
TGT_TILES = NTGT // LANES
BLUR = 0.1
LOG2E = 1.4426950408889634
KAPPA = LOG2E / BLUR
UNKAPPA = 1.0 / KAPPA
WIDTH = 256
f32 = jnp.float32
bf16 = jnp.bfloat16

SINE = (6.28318530707259, -41.34170211699658, 81.6052262062997, -76.7042813207251, 42.00980570831026, -14.394135222236105)


def split(x):
    hi = x.astype(bf16)
    lo = (x - hi.astype(f32)).astype(bf16)
    return hi, lo


def pieces(x):
    first = x.astype(bf16).astype(f32)
    rest = x - first
    second = rest.astype(bf16).astype(f32)
    return first, second, rest - second


def column_of(values, kind):
    sub = lax.broadcasted_iota(jnp.int32, (8, LANES), 0)
    groups = []
    for g in range(DIM // 8):
        v = jnp.full((8, LANES), values[8 * g], kind)
        for s in range(1, 8):
            v = jnp.where(sub == s, values[8 * g + s], v)
        groups.append(v)
    return jnp.concatenate(groups, 0)


def sine_turns(u):
    r = u - jnp.floor(u + 0.5)
    a = jnp.abs(r)
    b = jnp.minimum(a, 0.5 - a)
    z = b * b
    p = jnp.full_like(z, SINE[-1])
    for c in SINE[-2::-1]:
        p = p * z + c
    v = b * p
    return jnp.where(r < 0, -v, v)


def place_terms(a_ref, d_ref, rows, tiles):
    d_ref[...] = jnp.zeros_like(d_ref)
    for k, piece in enumerate(pieces(rows)):
        d_ref[:, k, :] = piece
    for t in range(tiles):
        a_ref[LANES * t : LANES * (t + 1), LANES : LANES + 8] = d_ref[t].T.astype(bf16)


def fill_left(a_ref, half):
    lane = lax.broadcasted_iota(jnp.int32, half.shape, 1)
    a_ref[:, :LANES] = half
    a_ref[:, LANES:] = jnp.where(lane < 64, jnp.zeros_like(half), half)


def log_sums(a_ref, b_ref, out):
    count = b_ref.shape[1] // WIDTH

    for n in range(count):
        s = jnp.dot(a_ref[...], b_ref[:, WIDTH * n : WIDTH * (n + 1)], preferred_element_type=f32)
        top = jnp.max(s, 0, keepdims=True)
        row = top + jnp.log2(jnp.sum(jnp.exp2(s - top), 0, keepdims=True))
        for k in range(WIDTH // LANES):
            r = n * (WIDTH // LANES) + k
            out[r : r + 1, :] = row[:, LANES * k : LANES * (k + 1)]


def merged(parts):
    top = jnp.max(parts, 0)
    return top + jnp.log2(jnp.sum(jnp.exp2(parts - top[None]), 0))


def ones_rows():
    row = lax.broadcasted_iota(jnp.int32, (64, LANES), 0)
    return jnp.where(row < 3, 1.0, 0.0).astype(bf16)


def first_rows(gen, shift, t_ref, w_ref, half_ref, b_ref, c_ref, far_ref, near_ref, out_ref, a_ref, d_ref, l_ref):
    offset = lax.axis_index("src") * NSRC
    modulus = NSRC * lax.axis_size("src")
    g = column_of(gen, jnp.int32)
    sh = column_of(shift, f32)
    lane = lax.broadcasted_iota(jnp.int32, (DIM, LANES), 1)
    phase = ((offset + lane) * g) & (modulus - 1)
    step = (LANES * g) & (modulus - 1)
    ones = ones_rows()
    for t in range(SRC_TILES):
        cols = slice(LANES * t, LANES * (t + 1))
        points = sine_turns(phase.astype(f32) * (1.0 / modulus) + sh)
        near_ref[t : t + 1, :] = 0.5 * jnp.sum(points * points, 0, keepdims=True)
        hi, lo = split(points * KAPPA)
        b_ref[0:64, cols] = hi
        b_ref[64:128, cols] = hi
        b_ref[128:192, cols] = ones
        b_ref[192:256, cols] = lo
        phase = (phase + step) & (modulus - 1)
    w = w_ref[...] * LOG2E
    c_ref[...] = w
    for t in range(TGT_TILES):
        rows = slice(LANES * t, LANES * (t + 1))
        y = t_ref[:, rows]
        far_ref[t : t + 1, :] = 0.5 * jnp.sum(y * y, 0, keepdims=True)
        hi = y.astype(bf16).astype(f32)
        half_ref[rows, :] = jnp.concatenate([y - hi, hi], 0).T.astype(bf16)
    fill_left(a_ref, half_ref[...])
    place_terms(a_ref, d_ref, w - KAPPA * far_ref[...], TGT_TILES)
    top = jnp.max(w, keepdims=True)
    total = top + jnp.log2(jnp.sum(jnp.exp2(w - top), keepdims=True))
    l_ref[SRC_TILES:, :] = jnp.broadcast_to(total, (8, LANES))
    log_sums(a_ref, b_ref, l_ref)
    out_ref[...] = jnp.broadcast_to(l_ref[...][None], out_ref.shape)


def source_side(b_ref, t_ref, half_ref, out_ref):
    for t in range(SRC_TILES):
        cols = slice(LANES * t, LANES * (t + 1))
        both = jnp.concatenate([b_ref[192:256, cols], b_ref[0:64, cols]], 0).astype(f32)
        half_ref[cols, :] = both.T.astype(bf16)
    ones = ones_rows()
    for t in range(TGT_TILES):
        cols = slice(LANES * t, LANES * (t + 1))
        hi, lo = split(t_ref[:, cols])
        out_ref[0:64, cols] = hi
        out_ref[64:128, cols] = hi
        out_ref[128:192, cols] = ones
        out_ref[192:256, cols] = lo


def first_columns(parts_ref, half_ref, b_ref, norm_ref, out_ref, a_ref, d_ref, l_ref):
    every = merged(parts_ref[...])
    norm = every[SRC_TILES:, :]
    norm_ref[...] = norm
    rows = (norm[0:1, :] - every[:SRC_TILES, :]) - math.log2(NSRC * lax.axis_size("src"))
    fill_left(a_ref, half_ref[...])
    place_terms(a_ref, d_ref, rows, SRC_TILES)
    log_sums(a_ref, b_ref, l_ref)
    out_ref[...] = jnp.broadcast_to(l_ref[...][None], out_ref.shape)


def later_rows(parts_ref, half_ref, b_ref, c_ref, out_ref, a_ref, d_ref, l_ref):
    rows = c_ref[...] - merged(parts_ref[...])
    fill_left(a_ref, half_ref[...])
    place_terms(a_ref, d_ref, rows, TGT_TILES)
    log_sums(a_ref, b_ref, l_ref)
    out_ref[...] = jnp.broadcast_to(l_ref[...][None], out_ref.shape)


def later_columns(parts_ref, half_ref, b_ref, norm_ref, near_ref, f_ref, out_ref, a_ref, d_ref, l_ref):
    every = merged(parts_ref[...]) - norm_ref[0:1, :]
    f_ref[...] = near_ref[...] - UNKAPPA * every
    fill_left(a_ref, half_ref[...])
    place_terms(a_ref, d_ref, -math.log2(NSRC * lax.axis_size("src")) - every, SRC_TILES)
    log_sums(a_ref, b_ref, l_ref)
    out_ref[...] = jnp.broadcast_to(l_ref[...][None], out_ref.shape)


def last_columns(parts_ref, far_ref, g_ref):
    g_ref[...] = far_ref[...] - UNKAPPA * merged(parts_ref[...])


def shape(dims, kind=f32):
    return jax.ShapeDtypeStruct(dims, kind)


def call(body, outs, inputs, scratch=(), smem=0):
    specs = [pl.BlockSpec(memory_space=pltpu.SMEM)] * smem
    specs += [pl.BlockSpec(memory_space=pltpu.VMEM)] * (len(inputs) - smem)
    return pl.pallas_call(
        body,
        out_shape=outs,
        in_specs=specs,
        out_specs=jax.tree.map(lambda _: pl.BlockSpec(memory_space=pltpu.VMEM), outs),
        scratch_shapes=scratch,
        name=body.__name__,
    )(*inputs)


def exchanged(x, axis):
    return lax.all_to_all(x, axis, split_axis=0, concat_axis=0, tiled=True)


def local(generator, shift, targets, log_weights):
    n_src, n_tgt = lax.axis_size("src"), lax.axis_size("tgt")
    f_tmp = lambda rows: [
        pltpu.VMEM((NTGT, 256), bf16),
        pltpu.VMEM((TGT_TILES, 8, LANES), f32),
        pltpu.VMEM((rows, LANES), f32),
    ]
    g_tmp = [
        pltpu.VMEM((NSRC, 256), bf16),
        pltpu.VMEM((SRC_TILES, 8, LANES), f32),
        pltpu.VMEM((TGT_TILES, LANES), f32),
    ]
    w = log_weights.reshape(TGT_TILES, LANES)
    f_half, f_right, c, far, near, part = call(
        first_rows,
        (
            shape((NTGT, LANES), bf16),
            shape((256, NSRC), bf16),
            shape((TGT_TILES, LANES)),
            shape((TGT_TILES, LANES)),
            shape((SRC_TILES, LANES)),
            shape((n_tgt, SRC_TILES + 8, LANES)),
        ),
        (generator, shift, targets, w),
        f_tmp(SRC_TILES + 8),
        smem=2,
    )
    got = exchanged(part, "tgt")
    g_half, g_right = call(
        source_side, (shape((NSRC, LANES), bf16), shape((256, NTGT), bf16)), (f_right, targets)
    )
    norm, part = call(
        first_columns,
        (shape((8, LANES)), shape((n_src, TGT_TILES, LANES))),
        (got, g_half, g_right),
        g_tmp,
    )
    got = exchanged(part, "src")
    part = call(
        later_rows, shape((n_tgt, SRC_TILES, LANES)), (got, f_half, f_right, c), f_tmp(SRC_TILES)
    )
    got = exchanged(part, "tgt")
    f, part = call(
        later_columns,
        (shape((SRC_TILES, LANES)), shape((n_src, TGT_TILES, LANES))),
        (got, g_half, g_right, norm, near),
        g_tmp,
    )
    got = exchanged(part, "src")
    g = call(last_columns, shape((TGT_TILES, LANES)), (got, far))
    return f.reshape(NSRC), g.reshape(NTGT)


def solution(mesh):
    in_specs = (P(), P(), P(None, "tgt"), P("tgt"))
    out_specs = (P("src"), P("tgt"))
    return jax.shard_map(local, mesh=mesh, in_specs=in_specs, out_specs=out_specs, check_vma=False)
```

time: 184 us -> 81 us (0.44)
  matrix products: 47.9 us -> 0 us
  blocking collectives: 10.2 us -> 40.6 us
  waiting for transfers between devices: 36.7 us -> 7.74 us
  other arithmetic: 27 us -> 0 us
  Pallas kernels: 0 us -> 22.1 us
  local copies, waits for them, and re-layouts: 19.7 us -> 0.75 us
  starting transfers between devices: 25.8 us -> 8.59 us
  loops' own time: 11.1 us -> 0 us
  between operations: 5.09 us -> 0.64 us
    dot_general x16 -> x0, matrix products: 47.9 us -> none  [cost_block(): lax.dot_general(points, targets, (((0,), (0,)), ((), ())), precision=high...]
    all_to_all x1 -> x3, blocking collectives: 10.2 us -> 40.6 us  [exchanged(): return lax.all_to_all(x, axis, split_axis=0, concat_axis=0, tiled=True)]
    all_to_all x4 -> x1, waiting for transfers between devices: 36.7 us -> 7.74 us  [exchanged(): return lax.all_to_all(x, axis, split_axis=0, concat_axis=0, tiled=True)]
    pallas_call x0 -> x6, Pallas kernels: none -> 22.1 us  [call(): pl.pallas_call(body, out_shape=outs, in_specs=specs, out_specs=jax.tree.m...]
    reduce_sum x34 -> x0, other arithmetic: 22 us -> none  [the longest x16 12.4 us: cost_block(): near = 0.5 * jnp.sum(points * points, 0)]
    all_to_all x4 -> x1, starting transfers between devices: 25.8 us -> 8.59 us  [exchanged(): return lax.all_to_all(x, axis, split_axis=0, concat_axis=0, tiled=True)]
    another operation x4 -> x0, loops' own time: 11.1 us -> none  [the longest x2 5.63 us: local(): lax.scan(column_pass, start_carry, jnp.arange(count, dtype=jnp.int32))]
    dynamic_slice x24 -> x0, local copies, waits for them, and re-layouts: 10 us -> none  [the longest x16 9.38 us: local(): peaks, totals = lax.map(row_pass, jnp.arange(count, dtype=jnp.int32))]
  transfers between devices with their start and end apart: 4 -> 1, of which waited for: 4 -> 1; matrix products, arithmetic and copies ran while one was open for 1% -> 0% of each run, Pallas kernels for 0% -> 3%
where the time goes in v1:
time: 81 us; the launch traced here: 80.4 us
  blocking collectives  40.6 us (50%)
  Pallas kernels  22.1 us (27%)
  starting transfers between devices  8.59 us (11%)
  waiting for transfers between devices  7.74 us (10%)
    all_to_all x3, blocking collectives, exchanged(): return lax.all_to_all(x, axis, split_axis=0, concat_axis=0, tiled=True)  40.6 us
    pallas_call x6, Pallas kernels, call(): pl.pallas_call(body, out_shape=outs, in_specs=specs, out_specs=jax.tree.m...  22.1 us
    all_to_all x1, starting transfers between devices, exchanged(): return lax.all_to_all(x, axis, split_axis=0, concat_axis=0, tiled=True)  8.59 us
    all_to_all x1, waiting for transfers between devices, exchanged(): return lax.all_to_all(x, axis, split_axis=0, concat_axis=0, tiled=True)  7.74 us
  transfers between devices with their start and end apart: 1, of which 1 were waited for; matrix products, arithmetic and copies ran while one was open for 0% of the time, Pallas kernels for 3%

profile of v1, /device:TPU:1, one launch (start us, length us, event | category | flops | bytes accessed | tf_op | source)
XLA Modules:
  0.0 80.4 jit_solution(3542712240600685973)
XLA Ops:
  0.6 4.6 %first_rows.1 = (bf16[1024,128]{1,0:T(8,128)(2,1)}, bf16[256,2048]{1,0:T(8,128)(2,1)}, f32[8,128]{1,0:T(8,128)}, f32[8,128]{1,0:T(8,128)}, f32[16,128]{1,0:T(8,128)}, /*index=5*/f32[32,24,128]{2,1,0:T(8,128)}) custom-call(s32[64]{0:T(128)} %gen.1, f32[64]{0:T(128)} %shift.1, f32[64,1024]{1,0:T(8,128)} %t_ref.3, f32[8,128]{1,0:T(8,128)} %bitcast.3), custom_call_target="tpu_custom_call" | custom-call | tf_op jit(solution)/shard_map/first_rows/pallas_call | solution.py:188
  5.3 8.6 %all-to-all-start = ((f32[32,24,128]{2,1,0:T(8,128)}), f32[32,24,128]{2,1,0:T(8,128)S(1)}, u32[]{:S(2)}, u32[]{:S(2)}) async-start(f32[32,24,128]{2,1,0:T(8,128)} %get-tuple-element.14), calls=%async_computation | async-start | bytes 786432 | tf_op jit(solution)/shard_map/all_to_all | solution.py:199
  13.9 2.5 %source_side.1 = (bf16[2048,128]{1,0:T(8,128)(2,1)}, bf16[256,1024]{1,0:T(8,128)(2,1)}) custom-call(bf16[256,2048]{1,0:T(8,128)(2,1)} %get-tuple-element.15.b_ref, f32[64,1024]{1,0:T(8,128)} %t_ref.3), custom_call_target="tpu_custom_call" | custom-call | tf_op jit(solution)/shard_map/source_side/pallas_call | solution.py:188
  16.4 7.7 %all-to-all-done.parts_ref = f32[32,24,128]{2,1,0:T(8,128)S(1)} async-done(((f32[32,24,128]{2,1,0:T(8,128)}), f32[32,24,128]{2,1,0:T(8,128)S(1)}, u32[]{:S(2)}, u32[]{:S(2)}) %all-to-all-start) | async-done | bytes 393248 | tf_op jit(solution)/shard_map/all_to_all | solution.py:199
  24.1 0.0 copy-start
  24.1 0.7 copy-done
  24.9 4.6 %first_columns.1 = (f32[8,128]{1,0:T(8,128)}, f32[8,8,128]{2,1,0:T(8,128)}) custom-call(f32[32,24,128]{2,1,0:T(8,128)} %copy-done, bf16[2048,128]{1,0:T(8,128)(2,1)} %get-tuple-element.16.half_ref, bf16[256,1024]{1,0:T(8,128)(2,1)} %get-tuple-element.17.b_ref), custom_call_target="tpu_custom_call" | custom-call | tf_op jit(solution)/shard_map/first_columns/pallas_call | solution.py:188
  29.5 15.1 %all_to_all.20.parts_ref = f32[8,8,128]{2,1,0:T(8,128)} all-to-all(f32[8,8,128]{2,1,0:T(8,128)} %get-tuple-element.18), channel_id=1, replica_groups=mesh['src'=8,'tgt'=32] {'src'}, dimensions={0} | all-to-all | bytes 65536 | tf_op jit(solution)/shard_map/all_to_all | solution.py:199
  44.6 4.4 %later_rows.1 = f32[32,16,128]{2,1,0:T(8,128)} custom-call(f32[8,8,128]{2,1,0:T(8,128)} %all_to_all.20.parts_ref, bf16[1024,128]{1,0:T(8,128)(2,1)} %get-tuple-element.19.half_ref, bf16[256,2048]{1,0:T(8,128)(2,1)} %get-tuple-element.15.b_ref, f32[8,128]{1,0:T(8,128)} %get-tuple-element.20.c_ref), custom_call_target="tpu_custom_call" | custom-call | tf_op jit(solution)/shard_map/later_rows/pallas_call | solution.py:188
  49.0 14.7 %all_to_all.21.parts_ref = f32[32,16,128]{2,1,0:T(8,128)} all-to-all(f32[32,16,128]{2,1,0:T(8,128)} %later_rows.1), channel_id=1, replica_groups=mesh['src'=8,'tgt'=32] {'tgt'}, dimensions={0} | all-to-all | bytes 524288 | tf_op jit(solution)/shard_map/all_to_all | solution.py:199
  63.7 4.5 %later_columns.1 = (f32[16,128]{1,0:T(8,128)}, f32[8,8,128]{2,1,0:T(8,128)}) custom-call(f32[32,16,128]{2,1,0:T(8,128)} %all_to_all.21.parts_ref, bf16[2048,128]{1,0:T(8,128)(2,1)} %get-tuple-element.16.half_ref, bf16[256,1024]{1,0:T(8,128)(2,1)} %get-tuple-element.17.b_ref, f32[8,128]{1,0:T(8,128)} %get-tuple-element.21.norm_ref, ...), custom_call_target="tpu_custom_call" | custom-call | tf_op jit(solution)/shard_map/later_columns/pallas_call | solution.py:188
  68.2 10.8 %all_to_all.22.parts_ref = f32[8,8,128]{2,1,0:T(8,128)} all-to-all(f32[8,8,128]{2,1,0:T(8,128)} %get-tuple-element.24), channel_id=1, replica_groups=mesh['src'=8,'tgt'=32] {'src'}, dimensions={0} | all-to-all | bytes 65536 | tf_op jit(solution)/shard_map/all_to_all | solution.py:199
  79.0 1.4 %last_columns.1 = f32[8,128]{1,0:T(8,128)} custom-call(f32[8,8,128]{2,1,0:T(8,128)} %all_to_all.22.parts_ref, f32[8,128]{1,0:T(8,128)} %get-tuple-element.25.far_ref), custom_call_target="tpu_custom_call" | custom-call | tf_op jit(solution)/shard_map/last_columns/pallas_call | solution.py:188
Async XLA Ops:
  5.3 18.9 %all-to-all-start = ((f32[32,24,128]{2,1,0:T(8,128)}), f32[32,24,128]{2,1,0:T(8,128)S(1)}, u32[]{:S(2)}, u32[]{:S(2)}) async-start(f32[32,24,128]{2,1,0:T(8,128)} %get-tuple-element.14), calls=%async_computation | async-start | bytes 786432 | tf_op jit(solution)/shard_map/all_to_all | solution.py:199
  24.1 0.8 copy-start

commit v2 on v1

--- a/solution.py
+++ b/solution.py
@@ -17,6 +17,7 @@
 KAPPA = LOG2E / BLUR
 UNKAPPA = 1.0 / KAPPA
 WIDTH = 256
+GRANT = 16 * 2**20
 f32 = jnp.float32
 bf16 = jnp.bfloat16
 
@@ -192,6 +193,7 @@
         out_specs=jax.tree.map(lambda _: pl.BlockSpec(memory_space=pltpu.VMEM), outs),
         scratch_shapes=scratch,
         name=body.__name__,
+        compiler_params=pltpu.CompilerParams(vmem_limit_bytes=GRANT),
     )(*inputs)
 
 

time: 81 us -> 73.1 us (0.902)
  Pallas kernels: 22.1 us -> 13.2 us
  blocking collectives: 40.6 us -> 37.8 us
  waiting for transfers between devices: 7.74 us -> 10 us
  local copies, waits for them, and re-layouts: 0.75 us -> 2.3 us
    pallas_call x6, Pallas kernels: 22.1 us -> 13.2 us  [call(): pl.pallas_call(body, out_shape=outs, in_specs=specs, out_specs=jax.tree.m...]
    all_to_all x3, blocking collectives: 40.6 us -> 37.8 us  [exchanged(): return lax.all_to_all(x, axis, split_axis=0, concat_axis=0, tiled=True)]
    all_to_all x1, waiting for transfers between devices: 7.74 us -> 10 us  [exchanged(): return lax.all_to_all(x, axis, split_axis=0, concat_axis=0, tiled=True)]
    unnamed x2 -> x10, local copies, waits for them, and re-layouts: 0.75 us -> 2.3 us
  transfers between devices with their start and end apart: 1 -> 1, of which waited for: 1 -> 1; matrix products, arithmetic and copies ran while one was open for 0% -> 0% of each run, Pallas kernels for 3% -> 0%
where the time goes in v2:
time: 73.1 us; the launch traced here: 72.7 us
  blocking collectives  37.8 us (52%)
  Pallas kernels  13.2 us (18%)
  waiting for transfers between devices  10 us (14%)
  starting transfers between devices  8.71 us (12%)
  local copies, waits for them, and re-layouts  2.3 us (3%)
    all_to_all x3, blocking collectives, exchanged(): return lax.all_to_all(x, axis, split_axis=0, concat_axis=0, tiled=True)  37.8 us
    pallas_call x6, Pallas kernels, call(): pl.pallas_call(body, out_shape=outs, in_specs=specs, out_specs=jax.tree.m...  13.2 us
    all_to_all x1, waiting for transfers between devices, exchanged(): return lax.all_to_all(x, axis, split_axis=0, concat_axis=0, tiled=True)  10 us
    all_to_all x1, starting transfers between devices, exchanged(): return lax.all_to_all(x, axis, split_axis=0, concat_axis=0, tiled=True)  8.71 us
    unnamed x10, local copies, waits for them, and re-layouts  2.3 us
  transfers between devices with their start and end apart: 1, of which 1 were waited for; matrix products, arithmetic and copies ran while one was open for 0% of the time, Pallas kernels for 0%

profile of v2, /device:TPU:1, one launch (start us, length us, event | category | flops | bytes accessed | tf_op | source)
XLA Modules:
  0.0 72.7 jit_solution(9345024267879928013)
XLA Ops:
  0.6 0.0 copy-start.4
  0.6 0.0 copy-start.3
  0.6 0.6 copy-done.4
  1.3 0.0 copy-done.3
  1.3 0.0 copy-start
  1.3 0.9 %copy-done = f32[64,1024]{1,0:T(8,128)S(1)} copy-done((f32[64,1024]{1,0:T(8,128)S(1)}, f32[64,1024]{1,0:T(8,128)}, u32[]{:S(2)}) %copy-start) | copy-done | bytes 262168
  2.3 0.0 copy-start.2
  2.3 0.7 copy-done.2
  2.9 4.2 %first_rows.1 = (bf16[1024,128]{1,0:T(8,128)(2,1)S(1)}, bf16[256,2048]{1,0:T(8,128)(2,1)S(1)}, f32[8,128]{1,0:T(8,128)S(1)}, f32[8,128]{1,0:T(8,128)S(1)}, f32[1...) custom-call(s32[64]{0:T(128)S(1)} %copy-done.3, f32[64]{0:T(128)S(1)} %copy-done.4, f32[64,1024]{1,0:T(8,128)S(1)} %copy-done, ...), custom_call_target="tpu_custom_call" | custom-call | tf_op jit(solution)/shard_map/first_rows/pallas_call | solution.py:189
  7.2 0.0 copy-start.1
  7.2 8.7 %all-to-all-start = ((f32[32,24,128]{2,1,0:T(8,128)}), f32[32,24,128]{2,1,0:T(8,128)S(1)}, u32[]{:S(2)}, u32[]{:S(2)}) async-start(f32[32,24,128]{2,1,0:T(8,128)} %get-tuple-element.14), calls=%async_computation | async-start | bytes 786432 | tf_op jit(solution)/shard_map/all_to_all | solution.py:201
  15.9 0.0 copy-done.1
  15.9 0.3 source_side.1
  16.2 10.0 %all-to-all-done.parts_ref = f32[32,24,128]{2,1,0:T(8,128)S(1)} async-done(((f32[32,24,128]{2,1,0:T(8,128)}), f32[32,24,128]{2,1,0:T(8,128)S(1)}, u32[]{:S(2)}, u32[]{:S(2)}) %all-to-all-start) | async-done | bytes 393248 | tf_op jit(solution)/shard_map/all_to_all | solution.py:201
  26.2 2.6 %first_columns.1 = (f32[8,128]{1,0:T(8,128)S(1)}, f32[8,8,128]{2,1,0:T(8,128)S(1)}) custom-call(f32[32,24,128]{2,1,0:T(8,128)S(1)} %all-to-all-done.parts_ref, bf16[2048,128]{1,0:T(8,128)(2,1)S(1)} %get-tuple-element.16.half_ref, bf16[256,1024]{1,0:T(8,128)(2,1)S(1)} %get-tuple-element.17.b_ref), custom_call_target="tpu_custom_call" | custom-call | tf_op jit(solution)/shard_map/first_columns/pallas_call | solution.py:189
  28.8 14.8 %all_to_all.20.parts_ref = f32[8,8,128]{2,1,0:T(8,128)S(1)} all-to-all(f32[8,8,128]{2,1,0:T(8,128)S(1)} %get-tuple-element.18), channel_id=1, replica_groups=mesh['src'=8,'tgt'=32] {'src'}, dimensions={0} | all-to-all | bytes 65536 | tf_op jit(solution)/shard_map/all_to_all | solution.py:201
  43.6 2.3 %later_rows.1 = f32[32,16,128]{2,1,0:T(8,128)S(1)} custom-call(f32[8,8,128]{2,1,0:T(8,128)S(1)} %all_to_all.20.parts_ref, bf16[1024,128]{1,0:T(8,128)(2,1)S(1)} %get-tuple-element.19.half_ref, bf16[256,2048]{1,0:T(8,128)(2,1)S(1)} %get-tuple-element.15.b_ref, f32[8,128]{1,0:T(8,128)S(1)} %get-tuple-element.20.c_ref), custom_call_target="tpu_custom_call" | custom-call | tf_op jit(solution)/shard_map/later_rows/pallas_call | solution.py:189
  45.9 13.8 %all_to_all.21.parts_ref = f32[32,16,128]{2,1,0:T(8,128)S(1)} all-to-all(f32[32,16,128]{2,1,0:T(8,128)S(1)} %later_rows.1), channel_id=1, replica_groups=mesh['src'=8,'tgt'=32] {'tgt'}, dimensions={0} | all-to-all | bytes 524288 | tf_op jit(solution)/shard_map/all_to_all | solution.py:201
  59.7 3.1 %later_columns.1 = (f32[16,128]{1,0:T(8,128)}, f32[8,8,128]{2,1,0:T(8,128)S(1)}) custom-call(f32[32,16,128]{2,1,0:T(8,128)S(1)} %all_to_all.21.parts_ref, bf16[2048,128]{1,0:T(8,128)(2,1)S(1)} %get-tuple-element.16.half_ref, bf16[256,1024]{1,0:T(8,128)(2,1)S(1)} %get-tuple-element.17.b_ref, f32[8,128]{1,0:T(8,128)S(1)} %get-tuple-element.21.norm_ref, ...), custom_call_target="tpu_custom_call" | custom-call | tf_op jit(solution)/shard_map/later_columns/pallas_call | solution.py:189
  62.9 9.2 %all_to_all.22.parts_ref = f32[8,8,128]{2,1,0:T(8,128)S(1)} all-to-all(f32[8,8,128]{2,1,0:T(8,128)S(1)} %get-tuple-element.24), channel_id=1, replica_groups=mesh['src'=8,'tgt'=32] {'src'}, dimensions={0} | all-to-all | bytes 65536 | tf_op jit(solution)/shard_map/all_to_all | solution.py:201
  72.1 0.6 last_columns.1
Async XLA Ops:
  0.6 0.7 copy-start.4
  0.6 0.7 copy-start.3
  1.3 0.9 %copy-start = (f32[64,1024]{1,0:T(8,128)S(1)}, f32[64,1024]{1,0:T(8,128)}, u32[]{:S(2)}) copy-start(f32[64,1024]{1,0:T(8,128)} %t_ref.3) | copy-start | bytes 786436
  2.3 0.7 copy-start.2
  7.2 8.7 %copy-start.1 = (f32[64,1024]{1,0:T(8,128)S(1)}, f32[64,1024]{1,0:T(8,128)}, u32[]{:S(2)}) copy-start(f32[64,1024]{1,0:T(8,128)} %t_ref.3) | copy-start | bytes 786436
  7.2 19.0 %all-to-all-start = ((f32[32,24,128]{2,1,0:T(8,128)}), f32[32,24,128]{2,1,0:T(8,128)S(1)}, u32[]{:S(2)}, u32[]{:S(2)}) async-start(f32[32,24,128]{2,1,0:T(8,128)} %get-tuple-element.14), calls=%async_computation | async-start | bytes 786432 | tf_op jit(solution)/shard_map/all_to_all | solution.py:201

commit v3 on v2

--- a/solution.py
+++ b/solution.py
@@ -17,6 +17,7 @@
 KAPPA = LOG2E / BLUR
 UNKAPPA = 1.0 / KAPPA
 WIDTH = 256
+ROWS = 64
 GRANT = 16 * 2**20
 f32 = jnp.float32
 bf16 = jnp.bfloat16
@@ -75,15 +76,20 @@
 
 
 def log_sums(a_ref, b_ref, out):
-    count = b_ref.shape[1] // WIDTH
-
-    for n in range(count):
+    for n in range(b_ref.shape[1] // WIDTH):
         s = jnp.dot(a_ref[...], b_ref[:, WIDTH * n : WIDTH * (n + 1)], preferred_element_type=f32)
-        top = jnp.max(s, 0, keepdims=True)
-        row = top + jnp.log2(jnp.sum(jnp.exp2(s - top), 0, keepdims=True))
-        for k in range(WIDTH // LANES):
+        found = [([], []) for _ in range(WIDTH // LANES)]
+        for m in range(0, s.shape[0], ROWS):
+            for k, (tops, sums) in enumerate(found):
+                block = s[m : m + ROWS, LANES * k : LANES * (k + 1)].reshape(ROWS // 8, 8, LANES)
+                top = jnp.max(block, 0)
+                tops.append(top)
+                sums.append(jnp.sum(jnp.exp2(block - top[None]), 0))
+        for k, (tops, sums) in enumerate(found):
+            tops, sums = jnp.concatenate(tops, 0), jnp.concatenate(sums, 0)
+            top = jnp.max(tops, 0, keepdims=True)
             r = n * (WIDTH // LANES) + k
-            out[r : r + 1, :] = row[:, LANES * k : LANES * (k + 1)]
+            out[r : r + 1, :] = top + jnp.log2(jnp.sum(sums * jnp.exp2(tops - top), 0, keepdims=True))
 
 
 def merged(parts):
@@ -96,25 +102,44 @@
     return jnp.where(row < 3, 1.0, 0.0).astype(bf16)
 
 
-def first_rows(gen, shift, t_ref, w_ref, half_ref, b_ref, c_ref, far_ref, near_ref, out_ref, a_ref, d_ref, l_ref):
+def first_rows(
+    gen_hbm, shift_hbm, t_hbm, w_hbm,
+    half_ref, b_ref, g_half_ref, g_b_ref, c_ref, far_ref, near_ref, out_ref,
+    a_ref, d_ref, l_ref, gen, shift, t_ref, w_ref, sems,
+):
+    moves = [
+        pltpu.make_async_copy(src, dst, sems.at[k])
+        for k, (src, dst) in enumerate(
+            ((gen_hbm, gen), (shift_hbm, shift), (t_hbm, t_ref), (w_hbm, w_ref))
+        )
+    ]
+    for move in moves:
+        move.start()
+    ones = ones_rows()
     offset = lax.axis_index("src") * NSRC
     modulus = NSRC * lax.axis_size("src")
+    moves[0].wait()
+    moves[1].wait()
     g = column_of(gen, jnp.int32)
     sh = column_of(shift, f32)
     lane = lax.broadcasted_iota(jnp.int32, (DIM, LANES), 1)
     phase = ((offset + lane) * g) & (modulus - 1)
     step = (LANES * g) & (modulus - 1)
-    ones = ones_rows()
     for t in range(SRC_TILES):
         cols = slice(LANES * t, LANES * (t + 1))
         points = sine_turns(phase.astype(f32) * (1.0 / modulus) + sh)
         near_ref[t : t + 1, :] = 0.5 * jnp.sum(points * points, 0, keepdims=True)
-        hi, lo = split(points * KAPPA)
-        b_ref[0:64, cols] = hi
-        b_ref[64:128, cols] = hi
+        scaled = points * KAPPA
+        hi = scaled.astype(bf16).astype(f32)
+        lo = scaled - hi
+        b_ref[0:64, cols] = hi.astype(bf16)
+        b_ref[64:128, cols] = hi.astype(bf16)
         b_ref[128:192, cols] = ones
-        b_ref[192:256, cols] = lo
+        b_ref[192:256, cols] = lo.astype(bf16)
+        g_half_ref[cols, :] = jnp.concatenate([lo, hi], 0).T.astype(bf16)
         phase = (phase + step) & (modulus - 1)
+    moves[2].wait()
+    moves[3].wait()
     w = w_ref[...] * LOG2E
     c_ref[...] = w
     for t in range(TGT_TILES):
@@ -123,35 +148,29 @@
         far_ref[t : t + 1, :] = 0.5 * jnp.sum(y * y, 0, keepdims=True)
         hi = y.astype(bf16).astype(f32)
         half_ref[rows, :] = jnp.concatenate([y - hi, hi], 0).T.astype(bf16)
+        g_b_ref[0:64, rows] = hi.astype(bf16)
+        g_b_ref[64:128, rows] = hi.astype(bf16)
+        g_b_ref[128:192, rows] = ones
+        g_b_ref[192:256, rows] = (y - hi).astype(bf16)
     fill_left(a_ref, half_ref[...])
     place_terms(a_ref, d_ref, w - KAPPA * far_ref[...], TGT_TILES)
     top = jnp.max(w, keepdims=True)
     total = top + jnp.log2(jnp.sum(jnp.exp2(w - top), keepdims=True))
+    log_sums(a_ref, b_ref, l_ref)
     l_ref[SRC_TILES:, :] = jnp.broadcast_to(total, (8, LANES))
-    log_sums(a_ref, b_ref, l_ref)
-    out_ref[...] = jnp.broadcast_to(l_ref[...][None], out_ref.shape)
-
-
-def source_side(b_ref, t_ref, half_ref, out_ref):
-    for t in range(SRC_TILES):
-        cols = slice(LANES * t, LANES * (t + 1))
-        both = jnp.concatenate([b_ref[192:256, cols], b_ref[0:64, cols]], 0).astype(f32)
-        half_ref[cols, :] = both.T.astype(bf16)
-    ones = ones_rows()
-    for t in range(TGT_TILES):
-        cols = slice(LANES * t, LANES * (t + 1))
-        hi, lo = split(t_ref[:, cols])
-        out_ref[0:64, cols] = hi
-        out_ref[64:128, cols] = hi
-        out_ref[128:192, cols] = ones
-        out_ref[192:256, cols] = lo
+    for t in range(SRC_TILES + 1):
+        row = jnp.broadcast_to(l_ref[t : t + 1, :], (out_ref.shape[0], LANES))
+        out_ref[:, 0, LANES * t : LANES * (t + 1)] = row
 
 
 def first_columns(parts_ref, half_ref, b_ref, norm_ref, out_ref, a_ref, d_ref, l_ref):
-    every = merged(parts_ref[...])
-    norm = every[SRC_TILES:, :]
-    norm_ref[...] = norm
-    rows = (norm[0:1, :] - every[:SRC_TILES, :]) - math.log2(NSRC * lax.axis_size("src"))
+    every = []
+    for t in range(SRC_TILES + 1):
+        parts = parts_ref[:, 0, LANES * t : LANES * (t + 1)]
+        top = jnp.max(parts, 0, keepdims=True)
+        every.append(top + jnp.log2(jnp.sum(jnp.exp2(parts - top), 0, keepdims=True)))
+    norm_ref[...] = jnp.broadcast_to(every[-1], norm_ref.shape)
+    rows = (every[-1] - jnp.concatenate(every[:-1], 0)) - math.log2(NSRC * lax.axis_size("src"))
     fill_left(a_ref, half_ref[...])
     place_terms(a_ref, d_ref, rows, SRC_TILES)
     log_sums(a_ref, b_ref, l_ref)
@@ -183,13 +202,11 @@
     return jax.ShapeDtypeStruct(dims, kind)
 
 
-def call(body, outs, inputs, scratch=(), smem=0):
-    specs = [pl.BlockSpec(memory_space=pltpu.SMEM)] * smem
-    specs += [pl.BlockSpec(memory_space=pltpu.VMEM)] * (len(inputs) - smem)
+def call(body, outs, inputs, scratch=(), space=pltpu.VMEM):
     return pl.pallas_call(
         body,
         out_shape=outs,
-        in_specs=specs,
+        in_specs=[pl.BlockSpec(memory_space=space)] * len(inputs),
         out_specs=jax.tree.map(lambda _: pl.BlockSpec(memory_space=pltpu.VMEM), outs),
         scratch_shapes=scratch,
         name=body.__name__,
@@ -214,24 +231,30 @@
         pltpu.VMEM((TGT_TILES, LANES), f32),
     ]
     w = log_weights.reshape(TGT_TILES, LANES)
-    f_half, f_right, c, far, near, part = call(
+    f_half, f_right, g_half, g_right, c, far, near, part = call(
         first_rows,
         (
             shape((NTGT, LANES), bf16),
             shape((256, NSRC), bf16),
+            shape((NSRC, LANES), bf16),
+            shape((256, NTGT), bf16),
             shape((TGT_TILES, LANES)),
             shape((TGT_TILES, LANES)),
             shape((SRC_TILES, LANES)),
-            shape((n_tgt, SRC_TILES + 8, LANES)),
+            shape((n_tgt, 1, (SRC_TILES + 1) * LANES)),
         ),
         (generator, shift, targets, w),
-        f_tmp(SRC_TILES + 8),
-        smem=2,
+        f_tmp(SRC_TILES + 8)
+        + [
+            pltpu.SMEM((DIM,), jnp.int32),
+            pltpu.SMEM((DIM,), f32),
+            pltpu.VMEM((DIM, NTGT), f32),
+            pltpu.VMEM((TGT_TILES, LANES), f32),
+            pltpu.SemaphoreType.DMA((4,)),
+        ],
+        space=pltpu.HBM,
     )
     got = exchanged(part, "tgt")
-    g_half, g_right = call(
-        source_side, (shape((NSRC, LANES), bf16), shape((256, NTGT), bf16)), (f_right, targets)
-    )
     norm, part = call(
         first_columns,
         (shape((8, LANES)), shape((n_src, TGT_TILES, LANES))),

time: 73.1 us -> 69.4 us (0.949)
  blocking collectives: 37.8 us -> 55.4 us
  waiting for transfers between devices: 10 us -> 0 us
  starting transfers between devices: 8.71 us -> 0 us
  Pallas kernels: 13.2 us -> 10.7 us
    all_to_all x3 -> x4, blocking collectives: 37.8 us -> 55.4 us  [exchanged(): return lax.all_to_all(x, axis, split_axis=0, concat_axis=0, tiled=True)]
    all_to_all x1 -> x0, waiting for transfers between devices: 10 us -> none  [exchanged(): return lax.all_to_all(x, axis, split_axis=0, concat_axis=0, tiled=True)]
    all_to_all x1 -> x0, starting transfers between devices: 8.71 us -> none  [exchanged(): return lax.all_to_all(x, axis, split_axis=0, concat_axis=0, tiled=True)]
    pallas_call x6 -> x5, Pallas kernels: 13.2 us -> 10.7 us  [call(): pl.pallas_call(body, out_shape=outs, in_specs=[pl.BlockSpec(memory_space=...]
    unnamed x10 -> x8, local copies, waits for them, and re-layouts: 2.3 us -> 2.29 us
  transfers between devices with their start and end apart: 1 -> 0, of which waited for: 1 -> 0; matrix products, arithmetic and copies ran while one was open for 0% -> 0% of each run, Pallas kernels for 0% -> 0%
where the time goes in v3:
time: 69.4 us; the launch traced here: 69.1 us
  blocking collectives  55.4 us (80%)
  Pallas kernels  10.7 us (15%)
  local copies, waits for them, and re-layouts  2.29 us (3%)
    all_to_all x4, blocking collectives, exchanged(): return lax.all_to_all(x, axis, split_axis=0, concat_axis=0, tiled=True)  55.4 us
    pallas_call x5, Pallas kernels, call(): pl.pallas_call(body, out_shape=outs, in_specs=[pl.BlockSpec(memory_space=...  10.7 us
    unnamed x8, local copies, waits for them, and re-layouts  2.29 us

profile of v3, /device:TPU:1, one launch (start us, length us, event | category | flops | bytes accessed | tf_op | source)
XLA Modules:
  0.0 69.1 jit_solution(1604081776640603015)
XLA Ops:
  0.6 0.0 copy-start.3
  0.6 0.0 copy-start.2
  0.7 0.6 copy-done.3
  1.3 0.0 copy-done.2
  1.3 0.0 copy-start
  1.3 0.9 %copy-done = f32[64,1024]{1,0:T(8,128)S(1)} copy-done((f32[64,1024]{1,0:T(8,128)S(1)}, f32[64,1024]{1,0:T(8,128)}, u32[]{:S(2)}) %copy-start) | copy-done | bytes 262168
  2.3 0.0 copy-start.1
  2.3 0.7 copy-done.1
  2.9 3.5 %first_rows.1 = (bf16[1024,128]{1,0:T(8,128)(2,1)S(1)}, bf16[256,2048]{1,0:T(8,128)(2,1)S(1)}, bf16[2048,128]{1,0:T(8,128)(2,1)S(1)}, bf16[256,1024]{1,0:T(8,128...) custom-call(s32[64]{0:T(128)S(1)} %copy-done.2, ...), custom_call_target="tpu_custom_call" | custom-call | tf_op jit(solution)/shard_map/first_rows/pallas_call | solution.py:206
  6.5 17.5 %all_to_all.20.parts_ref = f32[32,1,2176]{2,1,0:T(1,128)S(1)} all-to-all(f32[32,1,2176]{2,1,0:T(1,128)S(1)} %get-tuple-element.14), channel_id=1, replica_groups=mesh['src'=8,'tgt'=32] {'tgt'}, dimensions={0} | all-to-all | bytes 557056 | tf_op jit(solution)/shard_map/all_to_all | solution.py:218
  24.0 2.2 %first_columns.1 = (f32[8,128]{1,0:T(8,128)S(1)}, f32[8,8,128]{2,1,0:T(8,128)S(1)}) custom-call(f32[32,1,2176]{2,1,0:T(1,128)S(1)} %all_to_all.20.parts_ref, bf16[2048,128]{1,0:T(8,128)(2,1)S(1)} %get-tuple-element.15.half_ref, bf16[256,1024]{1,0:T(8,128)(2,1)S(1)} %get-tuple-element.16.b_ref), custom_call_target="tpu_custom_call" | custom-call | tf_op jit(solution)/shard_map/first_columns/pallas_call | solution.py:206
  26.2 14.9 %all_to_all.21.parts_ref = f32[8,8,128]{2,1,0:T(8,128)S(1)} all-to-all(f32[8,8,128]{2,1,0:T(8,128)S(1)} %get-tuple-element.17), channel_id=1, replica_groups=mesh['src'=8,'tgt'=32] {'src'}, dimensions={0} | all-to-all | bytes 65536 | tf_op jit(solution)/shard_map/all_to_all | solution.py:218
  41.1 1.9 %later_rows.1 = f32[32,16,128]{2,1,0:T(8,128)S(1)} custom-call(f32[8,8,128]{2,1,0:T(8,128)S(1)} %all_to_all.21.parts_ref, bf16[1024,128]{1,0:T(8,128)(2,1)S(1)} %get-tuple-element.18.half_ref, bf16[256,2048]{1,0:T(8,128)(2,1)S(1)} %get-tuple-element.19.b_ref, f32[8,128]{1,0:T(8,128)S(1)} %get-tuple-element.20.c_ref), custom_call_target="tpu_custom_call" | custom-call | tf_op jit(solution)/shard_map/later_rows/pallas_call | solution.py:206
  43.0 13.8 %all_to_all.22.parts_ref = f32[32,16,128]{2,1,0:T(8,128)S(1)} all-to-all(f32[32,16,128]{2,1,0:T(8,128)S(1)} %later_rows.1), channel_id=1, replica_groups=mesh['src'=8,'tgt'=32] {'tgt'}, dimensions={0} | all-to-all | bytes 524288 | tf_op jit(solution)/shard_map/all_to_all | solution.py:218
  56.8 2.5 %later_columns.1 = (f32[16,128]{1,0:T(8,128)}, f32[8,8,128]{2,1,0:T(8,128)S(1)}) custom-call(f32[32,16,128]{2,1,0:T(8,128)S(1)} %all_to_all.22.parts_ref, bf16[2048,128]{1,0:T(8,128)(2,1)S(1)} %get-tuple-element.15.half_ref, bf16[256,1024]{1,0:T(8,128)(2,1)S(1)} %get-tuple-element.16.b_ref, f32[8,128]{1,0:T(8,128)S(1)} %get-tuple-element.21.norm_ref, ...), custom_call_target="tpu_custom_call" | custom-call | tf_op jit(solution)/shard_map/later_columns/pallas_call | solution.py:206
  59.3 9.2 %all_to_all.23.parts_ref = f32[8,8,128]{2,1,0:T(8,128)S(1)} all-to-all(f32[8,8,128]{2,1,0:T(8,128)S(1)} %get-tuple-element.24), channel_id=1, replica_groups=mesh['src'=8,'tgt'=32] {'src'}, dimensions={0} | all-to-all | bytes 65536 | tf_op jit(solution)/shard_map/all_to_all | solution.py:218
  68.5 0.6 last_columns.1
Async XLA Ops:
  0.6 0.7 copy-start.3
  0.6 0.7 copy-start.2
  1.3 0.9 %copy-start = (f32[64,1024]{1,0:T(8,128)S(1)}, f32[64,1024]{1,0:T(8,128)}, u32[]{:S(2)}) copy-start(f32[64,1024]{1,0:T(8,128)} %t_hbm.1) | copy-start | bytes 786436
  2.3 0.7 copy-start.1

commit v4 on v3

--- a/solution.py
+++ b/solution.py
@@ -185,16 +185,17 @@
     out_ref[...] = jnp.broadcast_to(l_ref[...][None], out_ref.shape)
 
 
-def later_columns(parts_ref, half_ref, b_ref, norm_ref, near_ref, f_ref, out_ref, a_ref, d_ref, l_ref):
+def later_columns(parts_ref, half_ref, b_ref, norm_ref, every_ref, out_ref, a_ref, d_ref, l_ref):
     every = merged(parts_ref[...]) - norm_ref[0:1, :]
-    f_ref[...] = near_ref[...] - UNKAPPA * every
+    every_ref[...] = every
     fill_left(a_ref, half_ref[...])
     place_terms(a_ref, d_ref, -math.log2(NSRC * lax.axis_size("src")) - every, SRC_TILES)
     log_sums(a_ref, b_ref, l_ref)
     out_ref[...] = jnp.broadcast_to(l_ref[...][None], out_ref.shape)
 
 
-def last_columns(parts_ref, far_ref, g_ref):
+def last_columns(parts_ref, far_ref, every_ref, near_ref, f_ref, g_ref):
+    f_ref[...] = near_ref[...] - UNKAPPA * every_ref[...]
     g_ref[...] = far_ref[...] - UNKAPPA * merged(parts_ref[...])
 
 
@@ -203,6 +204,8 @@
 
 
 def call(body, outs, inputs, scratch=(), space=pltpu.VMEM):
+    if space is pltpu.HBM:
+        inputs = [pltpu.with_memory_space_constraint(x, space) for x in inputs]
     return pl.pallas_call(
         body,
         out_shape=outs,
@@ -266,14 +269,18 @@
         later_rows, shape((n_tgt, SRC_TILES, LANES)), (got, f_half, f_right, c), f_tmp(SRC_TILES)
     )
     got = exchanged(part, "tgt")
-    f, part = call(
+    every, part = call(
         later_columns,
         (shape((SRC_TILES, LANES)), shape((n_src, TGT_TILES, LANES))),
-        (got, g_half, g_right, norm, near),
+        (got, g_half, g_right, norm),
         g_tmp,
     )
     got = exchanged(part, "src")
-    g = call(last_columns, shape((TGT_TILES, LANES)), (got, far))
+    f, g = call(
+        last_columns,
+        (shape((SRC_TILES, LANES)), shape((TGT_TILES, LANES))),
+        (got, far, every, near),
+    )
     return f.reshape(NSRC), g.reshape(NTGT)
 
 

time: 69.4 us -> 66.6 us (0.960)
  local copies, waits for them, and re-layouts: 2.29 us -> 0 us
    unnamed x8 -> x0, local copies, waits for them, and re-layouts: 2.29 us -> none
where the time goes in v4:
time: 66.6 us; the launch traced here: 66.4 us
  blocking collectives  55.5 us (83%)
  Pallas kernels  10.3 us (15%)
    all_to_all x4, blocking collectives, exchanged(): return lax.all_to_all(x, axis, split_axis=0, concat_axis=0, tiled=True)  55.5 us
    pallas_call x5, Pallas kernels, call(): pl.pallas_call(body, out_shape=outs, in_specs=[pl.BlockSpec(memory_space=...  10.3 us

profile of v4, /device:TPU:1, one launch (start us, length us, event | category | flops | bytes accessed | tf_op | source)
XLA Modules:
  0.0 66.4 jit_solution(16258969610495756369)
XLA Ops:
  0.6 3.6 %first_rows.1 = (bf16[1024,128]{1,0:T(8,128)(2,1)S(1)}, bf16[256,2048]{1,0:T(8,128)(2,1)S(1)}, bf16[2048,128]{1,0:T(8,128)(2,1)S(1)}, bf16[256,1024]{1,0:T(8,128...) custom-call(s32[64]{0:T(128)} %gen_hbm.1, ...), custom_call_target="tpu_custom_call" | custom-call | tf_op jit(solution)/shard_map/first_rows/pallas_call | solution.py:209
  4.3 17.5 %all_to_all.20.parts_ref = f32[32,1,2176]{2,1,0:T(1,128)S(1)} all-to-all(f32[32,1,2176]{2,1,0:T(1,128)S(1)} %get-tuple-element.16), channel_id=1, replica_groups=mesh['src'=8,'tgt'=32] {'tgt'}, dimensions={0} | all-to-all | bytes 557056 | tf_op jit(solution)/shard_map/all_to_all | solution.py:221
  21.8 2.2 %first_columns.1 = (f32[8,128]{1,0:T(8,128)S(1)}, f32[8,8,128]{2,1,0:T(8,128)S(1)}) custom-call(f32[32,1,2176]{2,1,0:T(1,128)S(1)} %all_to_all.20.parts_ref, bf16[2048,128]{1,0:T(8,128)(2,1)S(1)} %get-tuple-element.17.half_ref, bf16[256,1024]{1,0:T(8,128)(2,1)S(1)} %get-tuple-element.18.b_ref), custom_call_target="tpu_custom_call" | custom-call | tf_op jit(solution)/shard_map/first_columns/pallas_call | solution.py:209
  24.0 14.9 %all_to_all.21.parts_ref = f32[8,8,128]{2,1,0:T(8,128)S(1)} all-to-all(f32[8,8,128]{2,1,0:T(8,128)S(1)} %get-tuple-element.19), channel_id=1, replica_groups=mesh['src'=8,'tgt'=32] {'src'}, dimensions={0} | all-to-all | bytes 65536 | tf_op jit(solution)/shard_map/all_to_all | solution.py:221
  38.9 1.8 %later_rows.1 = f32[32,16,128]{2,1,0:T(8,128)S(1)} custom-call(f32[8,8,128]{2,1,0:T(8,128)S(1)} %all_to_all.21.parts_ref, bf16[1024,128]{1,0:T(8,128)(2,1)S(1)} %get-tuple-element.20.half_ref, bf16[256,2048]{1,0:T(8,128)(2,1)S(1)} %get-tuple-element.21.b_ref, f32[8,128]{1,0:T(8,128)S(1)} %get-tuple-element.22.c_ref), custom_call_target="tpu_custom_call" | custom-call | tf_op jit(solution)/shard_map/later_rows/pallas_call | solution.py:209
  40.7 13.9 %all_to_all.22.parts_ref = f32[32,16,128]{2,1,0:T(8,128)S(1)} all-to-all(f32[32,16,128]{2,1,0:T(8,128)S(1)} %later_rows.1), channel_id=1, replica_groups=mesh['src'=8,'tgt'=32] {'tgt'}, dimensions={0} | all-to-all | bytes 524288 | tf_op jit(solution)/shard_map/all_to_all | solution.py:221
  54.6 1.9 %later_columns.1 = (f32[16,128]{1,0:T(8,128)S(1)}, f32[8,8,128]{2,1,0:T(8,128)S(1)}) custom-call(f32[32,16,128]{2,1,0:T(8,128)S(1)} %all_to_all.22.parts_ref, bf16[2048,128]{1,0:T(8,128)(2,1)S(1)} %get-tuple-element.17.half_ref, bf16[256,1024]{1,0:T(8,128)(2,1)S(1)} %get-tuple-element.18.b_ref, f32[8,128]{1,0:T(8,128)S(1)} %get-tuple-element.23.norm_ref), custom_call_target="tpu_custom_call" | custom-call | tf_op jit(solution)/shard_map/later_columns/pallas_call | solution.py:209
  56.5 9.2 %all_to_all.23.parts_ref = f32[8,8,128]{2,1,0:T(8,128)S(1)} all-to-all(f32[8,8,128]{2,1,0:T(8,128)S(1)} %get-tuple-element.24), channel_id=1, replica_groups=mesh['src'=8,'tgt'=32] {'src'}, dimensions={0} | all-to-all | bytes 65536 | tf_op jit(solution)/shard_map/all_to_all | solution.py:221
  65.7 0.6 last_columns.1

commit v5 on v4

--- a/solution.py
+++ b/solution.py
@@ -12,6 +12,7 @@
 LANES = 128
 SRC_TILES = NSRC // LANES
 TGT_TILES = NTGT // LANES
+FIRST_ROWS = SRC_TILES + 1
 BLUR = 0.1
 LOG2E = 1.4426950408889634
 KAPPA = LOG2E / BLUR
@@ -123,13 +124,13 @@
     g = column_of(gen, jnp.int32)
     sh = column_of(shift, f32)
     lane = lax.broadcasted_iota(jnp.int32, (DIM, LANES), 1)
-    phase = ((offset + lane) * g) & (modulus - 1)
-    step = (LANES * g) & (modulus - 1)
+    turns = (((offset + lane) * g) & (modulus - 1)).astype(f32) * (1.0 / modulus) + sh
+    step = ((LANES * g) & (modulus - 1)).astype(f32) * (1.0 / modulus)
+    scaled, other = KAPPA * sine_turns(turns), KAPPA * sine_turns(turns + 0.25)
+    step_sin, step_cos = sine_turns(step), sine_turns(step + 0.25)
     for t in range(SRC_TILES):
         cols = slice(LANES * t, LANES * (t + 1))
-        points = sine_turns(phase.astype(f32) * (1.0 / modulus) + sh)
-        near_ref[t : t + 1, :] = 0.5 * jnp.sum(points * points, 0, keepdims=True)
-        scaled = points * KAPPA
+        near_ref[t : t + 1, :] = (0.5 * UNKAPPA**2) * jnp.sum(scaled * scaled, 0, keepdims=True)
         hi = scaled.astype(bf16).astype(f32)
         lo = scaled - hi
         b_ref[0:64, cols] = hi.astype(bf16)
@@ -137,7 +138,7 @@
         b_ref[128:192, cols] = ones
         b_ref[192:256, cols] = lo.astype(bf16)
         g_half_ref[cols, :] = jnp.concatenate([lo, hi], 0).T.astype(bf16)
-        phase = (phase + step) & (modulus - 1)
+        scaled, other = scaled * step_cos + other * step_sin, other * step_cos - scaled * step_sin
     moves[2].wait()
     moves[3].wait()
     w = w_ref[...] * LOG2E
@@ -158,19 +159,19 @@
     total = top + jnp.log2(jnp.sum(jnp.exp2(w - top), keepdims=True))
     log_sums(a_ref, b_ref, l_ref)
     l_ref[SRC_TILES:, :] = jnp.broadcast_to(total, (8, LANES))
-    for t in range(SRC_TILES + 1):
-        row = jnp.broadcast_to(l_ref[t : t + 1, :], (out_ref.shape[0], LANES))
-        out_ref[:, 0, LANES * t : LANES * (t + 1)] = row
+    for d in range(0, out_ref.shape[0], FIRST_ROWS):
+        out_ref[d : d + FIRST_ROWS, :] = l_ref[:FIRST_ROWS, :]
 
 
 def first_columns(parts_ref, half_ref, b_ref, norm_ref, out_ref, a_ref, d_ref, l_ref):
-    every = []
-    for t in range(SRC_TILES + 1):
-        parts = parts_ref[:, 0, LANES * t : LANES * (t + 1)]
-        top = jnp.max(parts, 0, keepdims=True)
-        every.append(top + jnp.log2(jnp.sum(jnp.exp2(parts - top), 0, keepdims=True)))
-    norm_ref[...] = jnp.broadcast_to(every[-1], norm_ref.shape)
-    rows = (every[-1] - jnp.concatenate(every[:-1], 0)) - math.log2(NSRC * lax.axis_size("src"))
+    parts = [parts_ref[d : d + FIRST_ROWS, :] for d in range(0, parts_ref.shape[0], FIRST_ROWS)]
+    top = parts[0]
+    for part in parts[1:]:
+        top = jnp.maximum(top, part)
+    every = top + jnp.log2(sum(jnp.exp2(part - top) for part in parts))
+    norm = every[SRC_TILES:, :]
+    norm_ref[...] = jnp.broadcast_to(norm, norm_ref.shape)
+    rows = (norm - every[:SRC_TILES, :]) - math.log2(NSRC * lax.axis_size("src"))
     fill_left(a_ref, half_ref[...])
     place_terms(a_ref, d_ref, rows, SRC_TILES)
     log_sums(a_ref, b_ref, l_ref)
@@ -244,7 +245,7 @@
             shape((TGT_TILES, LANES)),
             shape((TGT_TILES, LANES)),
             shape((SRC_TILES, LANES)),
-            shape((n_tgt, 1, (SRC_TILES + 1) * LANES)),
+            shape((n_tgt * FIRST_ROWS, LANES)),
         ),
         (generator, shift, targets, w),
         f_tmp(SRC_TILES + 8)
@@ -257,7 +258,8 @@
         ],
         space=pltpu.HBM,
     )
-    got = exchanged(part, "tgt")
+    part = part.reshape(n_tgt, 1, FIRST_ROWS * LANES)
+    got = exchanged(part, "tgt").reshape(n_tgt * FIRST_ROWS, LANES)
     norm, part = call(
         first_columns,
         (shape((8, LANES)), shape((n_src, TGT_TILES, LANES))),

time: 66.6 us -> 66 us (level)
  no operation moved by 1% of the time
where the time goes in v5:
time: 66 us; the launch traced here: 65.7 us
  blocking collectives  55.4 us (84%)
  Pallas kernels  9.64 us (15%)
    all_to_all x4, blocking collectives, exchanged(): return lax.all_to_all(x, axis, split_axis=0, concat_axis=0, tiled=True)  55.4 us
    pallas_call x5, Pallas kernels, call(): pl.pallas_call(body, out_shape=outs, in_specs=[pl.BlockSpec(memory_space=...  9.64 us

profile of v5, /device:TPU:1, one launch (start us, length us, event | category | flops | bytes accessed | tf_op | source)
XLA Modules:
  0.0 65.7 jit_solution(12204248527999276289)
XLA Ops:
  0.6 3.3 %first_rows.1 = (bf16[1024,128]{1,0:T(8,128)(2,1)S(1)}, bf16[256,2048]{1,0:T(8,128)(2,1)S(1)}, bf16[2048,128]{1,0:T(8,128)(2,1)S(1)}, bf16[256,1024]{1,0:T(8,128...) custom-call(s32[64]{0:T(128)} %gen_hbm.1, ...), custom_call_target="tpu_custom_call" | custom-call | tf_op jit(solution)/shard_map/first_rows/pallas_call | solution.py:210
  3.9 17.5 %all_to_all.20 = f32[32,1,2176]{2,1,0:T(1,128)S(1)} all-to-all(f32[32,1,2176]{2,1,0:T(1,128)S(1)} %bitcast.6), channel_id=1, replica_groups=mesh['src'=8,'tgt'=32] {'tgt'}, dimensions={0} | all-to-all | bytes 557056 | tf_op jit(solution)/shard_map/all_to_all | solution.py:222
  21.4 2.0 %first_columns.1 = (f32[8,128]{1,0:T(8,128)S(1)}, f32[8,8,128]{2,1,0:T(8,128)S(1)}) custom-call(f32[544,128]{1,0:T(8,128)S(1)} %bitcast.5, bf16[2048,128]{1,0:T(8,128)(2,1)S(1)} %get-tuple-element.17.half_ref, bf16[256,1024]{1,0:T(8,128)(2,1)S(1)} %get-tuple-element.18.b_ref), custom_call_target="tpu_custom_call" | custom-call | tf_op jit(solution)/shard_map/first_columns/pallas_call | solution.py:210
  23.4 14.9 %all_to_all.21.parts_ref = f32[8,8,128]{2,1,0:T(8,128)S(1)} all-to-all(f32[8,8,128]{2,1,0:T(8,128)S(1)} %get-tuple-element.19), channel_id=1, replica_groups=mesh['src'=8,'tgt'=32] {'src'}, dimensions={0} | all-to-all | bytes 65536 | tf_op jit(solution)/shard_map/all_to_all | solution.py:222
  38.2 1.8 %later_rows.1 = f32[32,16,128]{2,1,0:T(8,128)S(1)} custom-call(f32[8,8,128]{2,1,0:T(8,128)S(1)} %all_to_all.21.parts_ref, bf16[1024,128]{1,0:T(8,128)(2,1)S(1)} %get-tuple-element.20.half_ref, bf16[256,2048]{1,0:T(8,128)(2,1)S(1)} %get-tuple-element.21.b_ref, f32[8,128]{1,0:T(8,128)S(1)} %get-tuple-element.22.c_ref), custom_call_target="tpu_custom_call" | custom-call | tf_op jit(solution)/shard_map/later_rows/pallas_call | solution.py:210
  40.1 13.8 %all_to_all.22.parts_ref = f32[32,16,128]{2,1,0:T(8,128)S(1)} all-to-all(f32[32,16,128]{2,1,0:T(8,128)S(1)} %later_rows.1), channel_id=1, replica_groups=mesh['src'=8,'tgt'=32] {'tgt'}, dimensions={0} | all-to-all | bytes 524288 | tf_op jit(solution)/shard_map/all_to_all | solution.py:222
  53.9 1.9 %later_columns.1 = (f32[16,128]{1,0:T(8,128)S(1)}, f32[8,8,128]{2,1,0:T(8,128)S(1)}) custom-call(f32[32,16,128]{2,1,0:T(8,128)S(1)} %all_to_all.22.parts_ref, bf16[2048,128]{1,0:T(8,128)(2,1)S(1)} %get-tuple-element.17.half_ref, bf16[256,1024]{1,0:T(8,128)(2,1)S(1)} %get-tuple-element.18.b_ref, f32[8,128]{1,0:T(8,128)S(1)} %get-tuple-element.23.norm_ref), custom_call_target="tpu_custom_call" | custom-call | tf_op jit(solution)/shard_map/later_columns/pallas_call | solution.py:210
  55.9 9.2 %all_to_all.23.parts_ref = f32[8,8,128]{2,1,0:T(8,128)S(1)} all-to-all(f32[8,8,128]{2,1,0:T(8,128)S(1)} %get-tuple-element.24), channel_id=1, replica_groups=mesh['src'=8,'tgt'=32] {'src'}, dimensions={0} | all-to-all | bytes 65536 | tf_op jit(solution)/shard_map/all_to_all | solution.py:222
  65.1 0.6 last_columns.1

commit v6 on v5

--- a/solution.py
+++ b/solution.py
@@ -20,6 +20,7 @@
 WIDTH = 256
 ROWS = 64
 GRANT = 16 * 2**20
+FIRST = {"src": 4, "tgt": 21}
 f32 = jnp.float32
 bf16 = jnp.bfloat16
 
@@ -67,18 +68,18 @@
     for k, piece in enumerate(pieces(rows)):
         d_ref[:, k, :] = piece
     for t in range(tiles):
-        a_ref[LANES * t : LANES * (t + 1), LANES : LANES + 8] = d_ref[t].T.astype(bf16)
+        a_ref[LANES * t : LANES * (t + 1), 0:8] = d_ref[t].T.astype(bf16)
 
 
 def fill_left(a_ref, half):
     lane = lax.broadcasted_iota(jnp.int32, half.shape, 1)
-    a_ref[:, :LANES] = half
-    a_ref[:, LANES:] = jnp.where(lane < 64, jnp.zeros_like(half), half)
-
-
-def log_sums(a_ref, b_ref, out):
+    a_ref[...] = jnp.where(lane < 64, jnp.zeros_like(half), half)
+
+
+def log_sums(half_ref, a_ref, b_ref, out):
     for n in range(b_ref.shape[1] // WIDTH):
-        s = jnp.dot(a_ref[...], b_ref[:, WIDTH * n : WIDTH * (n + 1)], preferred_element_type=f32)
+        a = jnp.concatenate([half_ref[...], a_ref[...]], 1)
+        s = jnp.dot(a, b_ref[:, WIDTH * n : WIDTH * (n + 1)], preferred_element_type=f32)
         found = [([], []) for _ in range(WIDTH // LANES)]
         for m in range(0, s.shape[0], ROWS):
             for k, (tops, sums) in enumerate(found):
@@ -157,7 +158,7 @@
     place_terms(a_ref, d_ref, w - KAPPA * far_ref[...], TGT_TILES)
     top = jnp.max(w, keepdims=True)
     total = top + jnp.log2(jnp.sum(jnp.exp2(w - top), keepdims=True))
-    log_sums(a_ref, b_ref, l_ref)
+    log_sums(half_ref, a_ref, b_ref, l_ref)
     l_ref[SRC_TILES:, :] = jnp.broadcast_to(total, (8, LANES))
     for d in range(0, out_ref.shape[0], FIRST_ROWS):
         out_ref[d : d + FIRST_ROWS, :] = l_ref[:FIRST_ROWS, :]
@@ -174,7 +175,7 @@
     rows = (norm - every[:SRC_TILES, :]) - math.log2(NSRC * lax.axis_size("src"))
     fill_left(a_ref, half_ref[...])
     place_terms(a_ref, d_ref, rows, SRC_TILES)
-    log_sums(a_ref, b_ref, l_ref)
+    log_sums(half_ref, a_ref, b_ref, l_ref)
     out_ref[...] = jnp.broadcast_to(l_ref[...][None], out_ref.shape)
 
 
@@ -182,7 +183,7 @@
     rows = c_ref[...] - merged(parts_ref[...])
     fill_left(a_ref, half_ref[...])
     place_terms(a_ref, d_ref, rows, TGT_TILES)
-    log_sums(a_ref, b_ref, l_ref)
+    log_sums(half_ref, a_ref, b_ref, l_ref)
     out_ref[...] = jnp.broadcast_to(l_ref[...][None], out_ref.shape)
 
 
@@ -191,7 +192,7 @@
     every_ref[...] = every
     fill_left(a_ref, half_ref[...])
     place_terms(a_ref, d_ref, -math.log2(NSRC * lax.axis_size("src")) - every, SRC_TILES)
-    log_sums(a_ref, b_ref, l_ref)
+    log_sums(half_ref, a_ref, b_ref, l_ref)
     out_ref[...] = jnp.broadcast_to(l_ref[...][None], out_ref.shape)
 
 
@@ -219,18 +220,22 @@
 
 
 def exchanged(x, axis):
-    return lax.all_to_all(x, axis, split_axis=0, concat_axis=0, tiled=True)
+    n, first = lax.axis_size(axis), FIRST[axis]
+    order = [(first + k) % n for k in range(n)]
+    return lax.all_to_all(
+        x, axis, split_axis=0, concat_axis=0, axis_index_groups=[order], tiled=True
+    )
 
 
 def local(generator, shift, targets, log_weights):
     n_src, n_tgt = lax.axis_size("src"), lax.axis_size("tgt")
     f_tmp = lambda rows: [
-        pltpu.VMEM((NTGT, 256), bf16),
+        pltpu.VMEM((NTGT, LANES), bf16),
         pltpu.VMEM((TGT_TILES, 8, LANES), f32),
         pltpu.VMEM((rows, LANES), f32),
     ]
     g_tmp = [
-        pltpu.VMEM((NSRC, 256), bf16),
+        pltpu.VMEM((NSRC, LANES), bf16),
         pltpu.VMEM((SRC_TILES, 8, LANES), f32),
         pltpu.VMEM((TGT_TILES, LANES), f32),
     ]

time: 66 us -> 58.5 us (0.89)
  blocking collectives: 55.4 us -> 47.9 us
    all_to_all x4, blocking collectives: 55.4 us -> 47.9 us  [exchanged(): lax.all_to_all(x, axis, split_axis=0, concat_axis=0, axis_index_groups=[o...]
where the time goes in v6:
time: 58.5 us; the launch traced here: 58.2 us
  blocking collectives  47.9 us (82%)
  Pallas kernels  9.66 us (17%)
  between operations  0.65 us (1%)
    all_to_all x4, blocking collectives, exchanged(): lax.all_to_all(x, axis, split_axis=0, concat_axis=0, axis_index_groups=[o...  47.9 us
    pallas_call x5, Pallas kernels, call(): pl.pallas_call(body, out_shape=outs, in_specs=[pl.BlockSpec(memory_space=...  9.66 us

profile of v6, /device:TPU:1, one launch (start us, length us, event | category | flops | bytes accessed | tf_op | source)
XLA Modules:
  0.0 58.2 jit_solution(12402737542534339069)
XLA Ops:
  0.6 3.2 %first_rows.1 = (bf16[1024,128]{1,0:T(8,128)(2,1)S(1)}, bf16[256,2048]{1,0:T(8,128)(2,1)S(1)}, bf16[2048,128]{1,0:T(8,128)(2,1)S(1)}, bf16[256,1024]{1,0:T(8,128...) custom-call(s32[64]{0:T(128)} %gen_hbm.1, ...), custom_call_target="tpu_custom_call" | custom-call | tf_op jit(solution)/shard_map/first_rows/pallas_call | solution.py:211
  3.9 13.9 %all_to_all.20 = f32[32,1,2176]{2,1,0:T(1,128)S(1)} all-to-all(f32[32,1,2176]{2,1,0:T(1,128)S(1)} %bitcast.6), channel_id=1, replica_groups={{21,22,23,24,25,26,27,28,29,30,31,0,1,2,3,4,5,6,7,8,9,10,11,12,13,14,15..., dimensions={0} | all-to-all | bytes 557056 | tf_op jit(solution)/shard_map/all_to_all | solution.py:225
  17.8 2.0 %first_columns.1 = (f32[8,128]{1,0:T(8,128)S(1)}, f32[8,8,128]{2,1,0:T(8,128)S(1)}) custom-call(f32[544,128]{1,0:T(8,128)S(1)} %bitcast.5, bf16[2048,128]{1,0:T(8,128)(2,1)S(1)} %get-tuple-element.17.half_ref, bf16[256,1024]{1,0:T(8,128)(2,1)S(1)} %get-tuple-element.18.b_ref), custom_call_target="tpu_custom_call" | custom-call | tf_op jit(solution)/shard_map/first_columns/pallas_call | solution.py:211
  19.8 11.6 %all_to_all.21.parts_ref = f32[8,8,128]{2,1,0:T(8,128)S(1)} all-to-all(f32[8,8,128]{2,1,0:T(8,128)S(1)} %get-tuple-element.19), channel_id=1, replica_groups={{128,160,192,224,0,32,64,96},{129,161,193,225,1,33,65,97},{130,162,194,..., dimensions={0} | all-to-all | bytes 65536 | tf_op jit(solution)/shard_map/all_to_all | solution.py:225
  31.4 1.8 %later_rows.1 = f32[32,16,128]{2,1,0:T(8,128)S(1)} custom-call(f32[8,8,128]{2,1,0:T(8,128)S(1)} %all_to_all.21.parts_ref, bf16[1024,128]{1,0:T(8,128)(2,1)S(1)} %get-tuple-element.20.half_ref, bf16[256,2048]{1,0:T(8,128)(2,1)S(1)} %get-tuple-element.21.b_ref, f32[8,128]{1,0:T(8,128)S(1)} %get-tuple-element.22.c_ref), custom_call_target="tpu_custom_call" | custom-call | tf_op jit(solution)/shard_map/later_rows/pallas_call | solution.py:211
  33.2 12.8 %all_to_all.22.parts_ref = f32[32,16,128]{2,1,0:T(8,128)S(1)} all-to-all(f32[32,16,128]{2,1,0:T(8,128)S(1)} %later_rows.1), channel_id=1, replica_groups={{21,22,23,24,25,26,27,28,29,30,31,0,1,2,3,4,5,6,7,8,9,10,11,12,13,14,15..., dimensions={0} | all-to-all | bytes 524288 | tf_op jit(solution)/shard_map/all_to_all | solution.py:225
  46.1 2.0 %later_columns.1 = (f32[16,128]{1,0:T(8,128)S(1)}, f32[8,8,128]{2,1,0:T(8,128)S(1)}) custom-call(f32[32,16,128]{2,1,0:T(8,128)S(1)} %all_to_all.22.parts_ref, bf16[2048,128]{1,0:T(8,128)(2,1)S(1)} %get-tuple-element.17.half_ref, bf16[256,1024]{1,0:T(8,128)(2,1)S(1)} %get-tuple-element.18.b_ref, f32[8,128]{1,0:T(8,128)S(1)} %get-tuple-element.23.norm_ref), custom_call_target="tpu_custom_call" | custom-call | tf_op jit(solution)/shard_map/later_columns/pallas_call | solution.py:211
  48.0 9.5 %all_to_all.23.parts_ref = f32[8,8,128]{2,1,0:T(8,128)S(1)} all-to-all(f32[8,8,128]{2,1,0:T(8,128)S(1)} %get-tuple-element.24), channel_id=1, replica_groups={{128,160,192,224,0,32,64,96},{129,161,193,225,1,33,65,97},{130,162,194,..., dimensions={0} | all-to-all | bytes 65536 | tf_op jit(solution)/shard_map/all_to_all | solution.py:225
  57.6 0.6 %last_columns.1 = (f32[16,128]{1,0:T(8,128)}, f32[8,128]{1,0:T(8,128)}) custom-call(f32[8,8,128]{2,1,0:T(8,128)S(1)} %all_to_all.23.parts_ref, f32[8,128]{1,0:T(8,128)S(1)} %get-tuple-element.25.far_ref, f32[16,128]{1,0:T(8,128)S(1)} %get-tuple-element.26.every_ref, f32[16,128]{1,0:T(8,128)S(1)} %get-tuple-element.27.near_ref), custom_call_target="tpu_custom_call" | custom-call | tf_op jit(solution)/shard_map/last_columns/pallas_call | solution.py:211

commit v7 on v6

--- a/solution.py
+++ b/solution.py
@@ -19,8 +19,9 @@
 UNKAPPA = 1.0 / KAPPA
 WIDTH = 256
 ROWS = 64
+EARLY = 4
 GRANT = 16 * 2**20
-FIRST = {"src": 4, "tgt": 21}
+ORDER = {"src": [4, 0, 1, 7, 2, 6, 3, 5], "tgt": [(21 + k) % 32 for k in range(32)]}
 f32 = jnp.float32
 bf16 = jnp.bfloat16
 
@@ -118,6 +119,10 @@
     for move in moves:
         move.start()
     ones = ones_rows()
+    for t in range(SRC_TILES):
+        b_ref[128:192, LANES * t : LANES * (t + 1)] = ones
+    for t in range(TGT_TILES):
+        g_b_ref[128:192, LANES * t : LANES * (t + 1)] = ones
     offset = lax.axis_index("src") * NSRC
     modulus = NSRC * lax.axis_size("src")
     moves[0].wait()
@@ -129,17 +134,19 @@
     step = ((LANES * g) & (modulus - 1)).astype(f32) * (1.0 / modulus)
     scaled, other = KAPPA * sine_turns(turns), KAPPA * sine_turns(turns + 0.25)
     step_sin, step_cos = sine_turns(step), sine_turns(step + 0.25)
-    for t in range(SRC_TILES):
+    def put(t, scaled, other):
         cols = slice(LANES * t, LANES * (t + 1))
         near_ref[t : t + 1, :] = (0.5 * UNKAPPA**2) * jnp.sum(scaled * scaled, 0, keepdims=True)
         hi = scaled.astype(bf16).astype(f32)
         lo = scaled - hi
         b_ref[0:64, cols] = hi.astype(bf16)
         b_ref[64:128, cols] = hi.astype(bf16)
-        b_ref[128:192, cols] = ones
         b_ref[192:256, cols] = lo.astype(bf16)
         g_half_ref[cols, :] = jnp.concatenate([lo, hi], 0).T.astype(bf16)
-        scaled, other = scaled * step_cos + other * step_sin, other * step_cos - scaled * step_sin
+        return scaled * step_cos + other * step_sin, other * step_cos - scaled * step_sin
+
+    for t in range(EARLY):
+        scaled, other = put(t, scaled, other)
     moves[2].wait()
     moves[3].wait()
     w = w_ref[...] * LOG2E
@@ -152,10 +159,11 @@
         half_ref[rows, :] = jnp.concatenate([y - hi, hi], 0).T.astype(bf16)
         g_b_ref[0:64, rows] = hi.astype(bf16)
         g_b_ref[64:128, rows] = hi.astype(bf16)
-        g_b_ref[128:192, rows] = ones
         g_b_ref[192:256, rows] = (y - hi).astype(bf16)
     fill_left(a_ref, half_ref[...])
     place_terms(a_ref, d_ref, w - KAPPA * far_ref[...], TGT_TILES)
+    for t in range(EARLY, SRC_TILES):
+        scaled, other = put(t, scaled, other)
     top = jnp.max(w, keepdims=True)
     total = top + jnp.log2(jnp.sum(jnp.exp2(w - top), keepdims=True))
     log_sums(half_ref, a_ref, b_ref, l_ref)
@@ -220,10 +228,8 @@
 
 
 def exchanged(x, axis):
-    n, first = lax.axis_size(axis), FIRST[axis]
-    order = [(first + k) % n for k in range(n)]
     return lax.all_to_all(
-        x, axis, split_axis=0, concat_axis=0, axis_index_groups=[order], tiled=True
+        x, axis, split_axis=0, concat_axis=0, axis_index_groups=[ORDER[axis]], tiled=True
     )
 
 

time: 58.5 us -> 58.2 us (level)
  no operation moved by 1% of the time
where the time goes in v7:
time: 58.2 us; the launch traced here: 57.8 us
  blocking collectives  47.5 us (82%)
  Pallas kernels  9.64 us (17%)
  between operations  0.65 us (1%)
    all_to_all x4, blocking collectives, exchanged(): lax.all_to_all(x, axis, split_axis=0, concat_axis=0, axis_index_groups=[O...  47.5 us
    pallas_call x5, Pallas kernels, call(): pl.pallas_call(body, out_shape=outs, in_specs=[pl.BlockSpec(memory_space=...  9.64 us

profile of v7, /device:TPU:1, one launch (start us, length us, event | category | flops | bytes accessed | tf_op | source)
XLA Modules:
  0.0 57.8 jit_solution(4209517986029119897)
XLA Ops:
  0.6 3.2 %first_rows.1 = (bf16[1024,128]{1,0:T(8,128)(2,1)S(1)}, bf16[256,2048]{1,0:T(8,128)(2,1)S(1)}, bf16[2048,128]{1,0:T(8,128)(2,1)S(1)}, bf16[256,1024]{1,0:T(8,128...) custom-call(s32[64]{0:T(128)} %gen_hbm.1, ...), custom_call_target="tpu_custom_call" | custom-call | tf_op jit(solution)/shard_map/first_rows/pallas_call | solution.py:219
  3.9 13.9 %all_to_all.20 = f32[32,1,2176]{2,1,0:T(1,128)S(1)} all-to-all(f32[32,1,2176]{2,1,0:T(1,128)S(1)} %bitcast.6), channel_id=1, replica_groups={{21,22,23,24,25,26,27,28,29,30,31,0,1,2,3,4,5,6,7,8,9,10,11,12,13,14,15..., dimensions={0} | all-to-all | bytes 557056 | tf_op jit(solution)/shard_map/all_to_all | solution.py:231
  17.8 2.0 %first_columns.1 = (f32[8,128]{1,0:T(8,128)S(1)}, f32[8,8,128]{2,1,0:T(8,128)S(1)}) custom-call(f32[544,128]{1,0:T(8,128)S(1)} %bitcast.5, bf16[2048,128]{1,0:T(8,128)(2,1)S(1)} %get-tuple-element.17.half_ref, bf16[256,1024]{1,0:T(8,128)(2,1)S(1)} %get-tuple-element.18.b_ref), custom_call_target="tpu_custom_call" | custom-call | tf_op jit(solution)/shard_map/first_columns/pallas_call | solution.py:219
  19.8 11.6 %all_to_all.21.parts_ref = f32[8,8,128]{2,1,0:T(8,128)S(1)} all-to-all(f32[8,8,128]{2,1,0:T(8,128)S(1)} %get-tuple-element.19), channel_id=1, replica_groups={{128,0,32,224,64,192,96,160},{129,1,33,225,65,193,97,161},{130,2,34,226..., dimensions={0} | all-to-all | bytes 65536 | tf_op jit(solution)/shard_map/all_to_all | solution.py:231
  31.3 1.8 %later_rows.1 = f32[32,16,128]{2,1,0:T(8,128)S(1)} custom-call(f32[8,8,128]{2,1,0:T(8,128)S(1)} %all_to_all.21.parts_ref, bf16[1024,128]{1,0:T(8,128)(2,1)S(1)} %get-tuple-element.20.half_ref, bf16[256,2048]{1,0:T(8,128)(2,1)S(1)} %get-tuple-element.21.b_ref, f32[8,128]{1,0:T(8,128)S(1)} %get-tuple-element.22.c_ref), custom_call_target="tpu_custom_call" | custom-call | tf_op jit(solution)/shard_map/later_rows/pallas_call | solution.py:219
  33.2 12.9 %all_to_all.22.parts_ref = f32[32,16,128]{2,1,0:T(8,128)S(1)} all-to-all(f32[32,16,128]{2,1,0:T(8,128)S(1)} %later_rows.1), channel_id=1, replica_groups={{21,22,23,24,25,26,27,28,29,30,31,0,1,2,3,4,5,6,7,8,9,10,11,12,13,14,15..., dimensions={0} | all-to-all | bytes 524288 | tf_op jit(solution)/shard_map/all_to_all | solution.py:231
  46.0 2.0 %later_columns.1 = (f32[16,128]{1,0:T(8,128)S(1)}, f32[8,8,128]{2,1,0:T(8,128)S(1)}) custom-call(f32[32,16,128]{2,1,0:T(8,128)S(1)} %all_to_all.22.parts_ref, bf16[2048,128]{1,0:T(8,128)(2,1)S(1)} %get-tuple-element.17.half_ref, bf16[256,1024]{1,0:T(8,128)(2,1)S(1)} %get-tuple-element.18.b_ref, f32[8,128]{1,0:T(8,128)S(1)} %get-tuple-element.23.norm_ref), custom_call_target="tpu_custom_call" | custom-call | tf_op jit(solution)/shard_map/later_columns/pallas_call | solution.py:219
  48.0 9.2 %all_to_all.23.parts_ref = f32[8,8,128]{2,1,0:T(8,128)S(1)} all-to-all(f32[8,8,128]{2,1,0:T(8,128)S(1)} %get-tuple-element.24), channel_id=1, replica_groups={{128,0,32,224,64,192,96,160},{129,1,33,225,65,193,97,161},{130,2,34,226..., dimensions={0} | all-to-all | bytes 65536 | tf_op jit(solution)/shard_map/all_to_all | solution.py:231
  57.2 0.6 %last_columns.1 = (f32[16,128]{1,0:T(8,128)}, f32[8,128]{1,0:T(8,128)}) custom-call(f32[8,8,128]{2,1,0:T(8,128)S(1)} %all_to_all.23.parts_ref, f32[8,128]{1,0:T(8,128)S(1)} %get-tuple-element.25.far_ref, f32[16,128]{1,0:T(8,128)S(1)} %get-tuple-element.26.every_ref, f32[16,128]{1,0:T(8,128)S(1)} %get-tuple-element.27.near_ref), custom_call_target="tpu_custom_call" | custom-call | tf_op jit(solution)/shard_map/last_columns/pallas_call | solution.py:219

commit v8 on v7

--- a/solution.py
+++ b/solution.py
@@ -19,6 +19,7 @@
 UNKAPPA = 1.0 / KAPPA
 WIDTH = 256
 ROWS = 64
+SPLIT = 4
 EARLY = 4
 GRANT = 16 * 2**20
 ORDER = {"src": [4, 0, 1, 7, 2, 6, 3, 5], "tgt": [(21 + k) % 32 for k in range(32)]}
@@ -110,12 +111,11 @@
     half_ref, b_ref, g_half_ref, g_b_ref, c_ref, far_ref, near_ref, out_ref,
     a_ref, d_ref, l_ref, gen, shift, t_ref, w_ref, sems,
 ):
-    moves = [
-        pltpu.make_async_copy(src, dst, sems.at[k])
-        for k, (src, dst) in enumerate(
-            ((gen_hbm, gen), (shift_hbm, shift), (t_hbm, t_ref), (w_hbm, w_ref))
-        )
-    ]
+    pairs = [(gen_hbm, gen), (shift_hbm, shift), (w_hbm, w_ref)]
+    for k in range(0, DIM, DIM // SPLIT):
+        rows = pl.ds(k, DIM // SPLIT)
+        pairs.append((t_hbm.at[rows], t_ref.at[rows]))
+    moves = [pltpu.make_async_copy(src, dst, sems.at[k]) for k, (src, dst) in enumerate(pairs)]
     for move in moves:
         move.start()
     ones = ones_rows()
@@ -147,8 +147,8 @@
 
     for t in range(EARLY):
         scaled, other = put(t, scaled, other)
-    moves[2].wait()
-    moves[3].wait()
+    for move in moves[2:]:
+        move.wait()
     w = w_ref[...] * LOG2E
     c_ref[...] = w
     for t in range(TGT_TILES):
@@ -265,7 +265,7 @@
             pltpu.SMEM((DIM,), f32),
             pltpu.VMEM((DIM, NTGT), f32),
             pltpu.VMEM((TGT_TILES, LANES), f32),
-            pltpu.SemaphoreType.DMA((4,)),
+            pltpu.SemaphoreType.DMA((3 + SPLIT,)),
         ],
         space=pltpu.HBM,
     )

time: 58.2 us -> 58.2 us (level)
  no operation moved by 1% of the time
where the time goes in v8:
time: 58.2 us; the launch traced here: 57.9 us
  blocking collectives  47.5 us (82%)
  Pallas kernels  9.68 us (17%)
  between operations  0.65 us (1%)
    all_to_all x4, blocking collectives, exchanged(): lax.all_to_all(x, axis, split_axis=0, concat_axis=0, axis_index_groups=[O...  47.5 us
    pallas_call x5, Pallas kernels, call(): pl.pallas_call(body, out_shape=outs, in_specs=[pl.BlockSpec(memory_space=...  9.68 us

profile of v8, /device:TPU:1, one launch (start us, length us, event | category | flops | bytes accessed | tf_op | source)
XLA Modules:
  0.0 57.9 jit_solution(4109368831797693961)
XLA Ops:
  0.6 3.3 %first_rows.1 = (bf16[1024,128]{1,0:T(8,128)(2,1)S(1)}, bf16[256,2048]{1,0:T(8,128)(2,1)S(1)}, bf16[2048,128]{1,0:T(8,128)(2,1)S(1)}, bf16[256,1024]{1,0:T(8,128...) custom-call(s32[64]{0:T(128)} %gen_hbm.1, ...), custom_call_target="tpu_custom_call" | custom-call | tf_op jit(solution)/shard_map/first_rows/pallas_call | solution.py:219
  3.9 13.9 %all_to_all.20 = f32[32,1,2176]{2,1,0:T(1,128)S(1)} all-to-all(f32[32,1,2176]{2,1,0:T(1,128)S(1)} %bitcast.6), channel_id=1, replica_groups={{21,22,23,24,25,26,27,28,29,30,31,0,1,2,3,4,5,6,7,8,9,10,11,12,13,14,15..., dimensions={0} | all-to-all | bytes 557056 | tf_op jit(solution)/shard_map/all_to_all | solution.py:231
  17.8 2.0 %first_columns.1 = (f32[8,128]{1,0:T(8,128)S(1)}, f32[8,8,128]{2,1,0:T(8,128)S(1)}) custom-call(f32[544,128]{1,0:T(8,128)S(1)} %bitcast.5, bf16[2048,128]{1,0:T(8,128)(2,1)S(1)} %get-tuple-element.17.half_ref, bf16[256,1024]{1,0:T(8,128)(2,1)S(1)} %get-tuple-element.18.b_ref), custom_call_target="tpu_custom_call" | custom-call | tf_op jit(solution)/shard_map/first_columns/pallas_call | solution.py:219
  19.8 11.5 %all_to_all.21.parts_ref = f32[8,8,128]{2,1,0:T(8,128)S(1)} all-to-all(f32[8,8,128]{2,1,0:T(8,128)S(1)} %get-tuple-element.19), channel_id=1, replica_groups={{128,0,32,224,64,192,96,160},{129,1,33,225,65,193,97,161},{130,2,34,226..., dimensions={0} | all-to-all | bytes 65536 | tf_op jit(solution)/shard_map/all_to_all | solution.py:231
  31.3 1.8 %later_rows.1 = f32[32,16,128]{2,1,0:T(8,128)S(1)} custom-call(f32[8,8,128]{2,1,0:T(8,128)S(1)} %all_to_all.21.parts_ref, bf16[1024,128]{1,0:T(8,128)(2,1)S(1)} %get-tuple-element.20.half_ref, bf16[256,2048]{1,0:T(8,128)(2,1)S(1)} %get-tuple-element.21.b_ref, f32[8,128]{1,0:T(8,128)S(1)} %get-tuple-element.22.c_ref), custom_call_target="tpu_custom_call" | custom-call | tf_op jit(solution)/shard_map/later_rows/pallas_call | solution.py:219
  33.2 12.9 %all_to_all.22.parts_ref = f32[32,16,128]{2,1,0:T(8,128)S(1)} all-to-all(f32[32,16,128]{2,1,0:T(8,128)S(1)} %later_rows.1), channel_id=1, replica_groups={{21,22,23,24,25,26,27,28,29,30,31,0,1,2,3,4,5,6,7,8,9,10,11,12,13,14,15..., dimensions={0} | all-to-all | bytes 524288 | tf_op jit(solution)/shard_map/all_to_all | solution.py:231
  46.1 2.0 %later_columns.1 = (f32[16,128]{1,0:T(8,128)S(1)}, f32[8,8,128]{2,1,0:T(8,128)S(1)}) custom-call(f32[32,16,128]{2,1,0:T(8,128)S(1)} %all_to_all.22.parts_ref, bf16[2048,128]{1,0:T(8,128)(2,1)S(1)} %get-tuple-element.17.half_ref, bf16[256,1024]{1,0:T(8,128)(2,1)S(1)} %get-tuple-element.18.b_ref, f32[8,128]{1,0:T(8,128)S(1)} %get-tuple-element.23.norm_ref), custom_call_target="tpu_custom_call" | custom-call | tf_op jit(solution)/shard_map/later_columns/pallas_call | solution.py:219
  48.0 9.2 %all_to_all.23.parts_ref = f32[8,8,128]{2,1,0:T(8,128)S(1)} all-to-all(f32[8,8,128]{2,1,0:T(8,128)S(1)} %get-tuple-element.24), channel_id=1, replica_groups={{128,0,32,224,64,192,96,160},{129,1,33,225,65,193,97,161},{130,2,34,226..., dimensions={0} | all-to-all | bytes 65536 | tf_op jit(solution)/shard_map/all_to_all | solution.py:231
  57.2 0.6 %last_columns.1 = (f32[16,128]{1,0:T(8,128)}, f32[8,128]{1,0:T(8,128)}) custom-call(f32[8,8,128]{2,1,0:T(8,128)S(1)} %all_to_all.23.parts_ref, f32[8,128]{1,0:T(8,128)S(1)} %get-tuple-element.25.far_ref, f32[16,128]{1,0:T(8,128)S(1)} %get-tuple-element.26.every_ref, f32[16,128]{1,0:T(8,128)S(1)} %get-tuple-element.27.near_ref), custom_call_target="tpu_custom_call" | custom-call | tf_op jit(solution)/shard_map/last_columns/pallas_call | solution.py:219

commit v9 on v7

--- a/solution.py
+++ b/solution.py
@@ -116,8 +116,8 @@
             ((gen_hbm, gen), (shift_hbm, shift), (t_hbm, t_ref), (w_hbm, w_ref))
         )
     ]
-    for move in moves:
-        move.start()
+    for k in (2, 0, 1, 3):
+        moves[k].start()
     ones = ones_rows()
     for t in range(SRC_TILES):
         b_ref[128:192, LANES * t : LANES * (t + 1)] = ones

time: 58.2 us -> 58.3 us (level)
  no operation moved by 1% of the time
where the time goes in v9:
time: 58.3 us; the launch traced here: 58 us
  blocking collectives  47.5 us (81%)
  Pallas kernels  9.77 us (17%)
  between operations  0.65 us (1%)
    all_to_all x4, blocking collectives, exchanged(): lax.all_to_all(x, axis, split_axis=0, concat_axis=0, axis_index_groups=[O...  47.5 us
    pallas_call x5, Pallas kernels, call(): pl.pallas_call(body, out_shape=outs, in_specs=[pl.BlockSpec(memory_space=...  9.77 us

profile of v9, /device:TPU:1, one launch (start us, length us, event | category | flops | bytes accessed | tf_op | source)
XLA Modules:
  0.0 58.0 jit_solution(1117073792027190543)
XLA Ops:
  0.6 3.4 %first_rows.1 = (bf16[1024,128]{1,0:T(8,128)(2,1)S(1)}, bf16[256,2048]{1,0:T(8,128)(2,1)S(1)}, bf16[2048,128]{1,0:T(8,128)(2,1)S(1)}, bf16[256,1024]{1,0:T(8,128...) custom-call(s32[64]{0:T(128)} %gen_hbm.1, ...), custom_call_target="tpu_custom_call" | custom-call | tf_op jit(solution)/shard_map/first_rows/pallas_call | solution.py:219
  4.0 13.9 %all_to_all.20 = f32[32,1,2176]{2,1,0:T(1,128)S(1)} all-to-all(f32[32,1,2176]{2,1,0:T(1,128)S(1)} %bitcast.6), channel_id=1, replica_groups={{21,22,23,24,25,26,27,28,29,30,31,0,1,2,3,4,5,6,7,8,9,10,11,12,13,14,15..., dimensions={0} | all-to-all | bytes 557056 | tf_op jit(solution)/shard_map/all_to_all | solution.py:231
  17.9 2.0 %first_columns.1 = (f32[8,128]{1,0:T(8,128)S(1)}, f32[8,8,128]{2,1,0:T(8,128)S(1)}) custom-call(f32[544,128]{1,0:T(8,128)S(1)} %bitcast.5, bf16[2048,128]{1,0:T(8,128)(2,1)S(1)} %get-tuple-element.17.half_ref, bf16[256,1024]{1,0:T(8,128)(2,1)S(1)} %get-tuple-element.18.b_ref), custom_call_target="tpu_custom_call" | custom-call | tf_op jit(solution)/shard_map/first_columns/pallas_call | solution.py:219
  19.9 11.6 %all_to_all.21.parts_ref = f32[8,8,128]{2,1,0:T(8,128)S(1)} all-to-all(f32[8,8,128]{2,1,0:T(8,128)S(1)} %get-tuple-element.19), channel_id=1, replica_groups={{128,0,32,224,64,192,96,160},{129,1,33,225,65,193,97,161},{130,2,34,226..., dimensions={0} | all-to-all | bytes 65536 | tf_op jit(solution)/shard_map/all_to_all | solution.py:231
  31.5 1.8 %later_rows.1 = f32[32,16,128]{2,1,0:T(8,128)S(1)} custom-call(f32[8,8,128]{2,1,0:T(8,128)S(1)} %all_to_all.21.parts_ref, bf16[1024,128]{1,0:T(8,128)(2,1)S(1)} %get-tuple-element.20.half_ref, bf16[256,2048]{1,0:T(8,128)(2,1)S(1)} %get-tuple-element.21.b_ref, f32[8,128]{1,0:T(8,128)S(1)} %get-tuple-element.22.c_ref), custom_call_target="tpu_custom_call" | custom-call | tf_op jit(solution)/shard_map/later_rows/pallas_call | solution.py:219
  33.3 12.9 %all_to_all.22.parts_ref = f32[32,16,128]{2,1,0:T(8,128)S(1)} all-to-all(f32[32,16,128]{2,1,0:T(8,128)S(1)} %later_rows.1), channel_id=1, replica_groups={{21,22,23,24,25,26,27,28,29,30,31,0,1,2,3,4,5,6,7,8,9,10,11,12,13,14,15..., dimensions={0} | all-to-all | bytes 524288 | tf_op jit(solution)/shard_map/all_to_all | solution.py:231
  46.2 2.0 %later_columns.1 = (f32[16,128]{1,0:T(8,128)S(1)}, f32[8,8,128]{2,1,0:T(8,128)S(1)}) custom-call(f32[32,16,128]{2,1,0:T(8,128)S(1)} %all_to_all.22.parts_ref, bf16[2048,128]{1,0:T(8,128)(2,1)S(1)} %get-tuple-element.17.half_ref, bf16[256,1024]{1,0:T(8,128)(2,1)S(1)} %get-tuple-element.18.b_ref, f32[8,128]{1,0:T(8,128)S(1)} %get-tuple-element.23.norm_ref), custom_call_target="tpu_custom_call" | custom-call | tf_op jit(solution)/shard_map/later_columns/pallas_call | solution.py:219
  48.1 9.2 %all_to_all.23.parts_ref = f32[8,8,128]{2,1,0:T(8,128)S(1)} all-to-all(f32[8,8,128]{2,1,0:T(8,128)S(1)} %get-tuple-element.24), channel_id=1, replica_groups={{128,0,32,224,64,192,96,160},{129,1,33,225,65,193,97,161},{130,2,34,226..., dimensions={0} | all-to-all | bytes 65536 | tf_op jit(solution)/shard_map/all_to_all | solution.py:231
  57.3 0.6 %last_columns.1 = (f32[16,128]{1,0:T(8,128)}, f32[8,128]{1,0:T(8,128)}) custom-call(f32[8,8,128]{2,1,0:T(8,128)S(1)} %all_to_all.23.parts_ref, f32[8,128]{1,0:T(8,128)S(1)} %get-tuple-element.25.far_ref, f32[16,128]{1,0:T(8,128)S(1)} %get-tuple-element.26.every_ref, f32[16,128]{1,0:T(8,128)S(1)} %get-tuple-element.27.near_ref), custom_call_target="tpu_custom_call" | custom-call | tf_op jit(solution)/shard_map/last_columns/pallas_call | solution.py:219
